TPU v7x, 32 devices: a whole 2x2x4 slice. The times are simulated.
32 devices in a mesh: groups: 2 (over y), ffn: 4 (over x, core), width: 4 (over z).
Axes of the slice: x: 2, y: 2, z: 4, core: 2. Of those that a mesh axis runs over, the one named last changes fastest.
Arguments:
- hidden: bfloat16 [2048, 8192], P(('groups', 'ffn'), 'width'), parts along dimension 0, may hold values from -8.4 to 8.4
- upstream: bfloat16 [2048, 8192], P(('groups', 'ffn'), 'width'), parts along dimension 0, may hold values from -6 to 6
- query_frozen_weight: bfloat16 [8192, 8192], P('width', 'ffn'), may hold values from -0.0625 to 0.0625
- key_value_frozen_weight: bfloat16 [2, 8192, 1024], P(None, 'width', 'ffn'), may hold values from -0.0625 to 0.0625
- output_frozen_weight: bfloat16 [8192, 8192], P('ffn', 'width'), may hold values from -0.0625 to 0.0625
- adapter_down: bfloat16 [6, 16, 8192], P('groups', None, 'width'), parts along dimension 0, may hold values from -0.0625 to 0.0625
- query_up_map: bfloat16 [32, 8192], P('groups', 'ffn'), parts along dimension 0, may hold values from -0.0625 to 0.0625
- key_value_up_maps: bfloat16 [4, 16, 1024], P('groups', None, 'ffn'), parts along dimension 0, may hold values from -0.0625 to 0.0625
- output_down_map: bfloat16 [32, 8192], P('groups', 'ffn'), parts along dimension 0, may hold values from -0.0625 to 0.0625
- output_up: bfloat16 [32, 8192], P('groups', 'width'), parts along dimension 0, may hold values from -0.0625 to 0.0625
Outputs:
- hidden_gradient: bfloat16 [2048, 8192], P(('groups', 'ffn'), 'width'), parts along dimension 0
- down_map_gradient: float32 [6, 16, 8192], P('groups', None, 'width'), parts along dimension 0
- query_up_map_gradient: float32 [32, 8192], P('groups', 'ffn'), parts along dimension 0
- key_value_up_maps_gradient: float32 [4, 16, 1024], P('groups', None, 'ffn'), parts along dimension 0
- output_down_map_gradient: float32 [32, 8192], P('groups', 'ffn'), parts along dimension 0
- output_up_map_gradient: float32 [32, 8192], P('groups', 'width'), parts along dimension 0
There are 2 independent parts, one for each index of `groups`. A program takes and returns all parts, laid end to end along the dimension named above; an argument that names none is the same for every part. Nothing has to cross between parts.
All inputs are finite; a program needn't handle non-finite values.
Results may differ from a plain program's by a relative error of at most 0.04.
Values may be sent and summed in bfloat16 or wider, within the bound.
A program may use at most 128 MiB of HBM per device.

v0:
```python
import math

import jax
import jax.numpy as jnp
from jax import lax
from jax.sharding import PartitionSpec as P

KV_HEADS = 8
HEAD_DIM = 128
ADAPTER_RANK = 16


adapter_scale = 2.0
rope_base = 500000.0


def from_partner(array, axis, bit):
    return lax.ppermute(array, axis, [(i, i ^ 1 << bit) for i in range(lax.axis_size(axis))])


def rotate(values, positions, first_dim, direction):
    columns = values.shape[1]
    head_dims = (first_dim + jnp.arange(columns, dtype=jnp.int32)) % HEAD_DIM
    pair_dims = head_dims - head_dims % 2
    frequency = jnp.exp(pair_dims.astype(jnp.float32) * (-math.log(rope_base) / HEAD_DIM))
    angles = positions.astype(jnp.float32)[:, None] * frequency[None, :]
    is_even = head_dims % 2 == 0
    following = jnp.roll(values, -1, axis=1)
    preceding = jnp.roll(values, 1, axis=1)
    partner = jnp.where(is_even[None, :], -following, preceding)
    return values * jnp.cos(angles) + direction * partner * jnp.sin(angles)


def contract_last(left_side, right_side):
    return lax.dot_general(
        left_side, right_side, (((1,), (1,)), ((), ())), preferred_element_type=jnp.float32
    )


def contract_leading(left_side, right_side):
    return lax.dot_general(
        left_side, right_side, (((0,), (0,)), ((), ())), preferred_element_type=jnp.float32
    )


def shards(
    hidden,
    upstream,
    query_frozen_weight,
    key_value_frozen_weight,
    output_frozen_weight,
    adapter_down,
    query_up_map,
    key_value_up_maps,
    output_down_map,
    output_up,
):
    ffn_count = lax.axis_size("ffn")
    width_count = lax.axis_size("width")
    ffn_index = lax.axis_index("ffn")
    width_index = lax.axis_index("width")
    hidden_rows_full, upstream_gradient_full = (
        lax.all_gather(hidden, "ffn", axis=0, tiled=True),
        lax.all_gather(upstream, "ffn", axis=0, tiled=True),
    )
    token_count = hidden_rows_full.shape[0]
    query_rows = token_count // width_count
    query_cols = query_frozen_weight.shape[1]
    key_cols = key_value_frozen_weight.shape[2]
    row_start = width_index * query_rows
    positions = jnp.arange(token_count, dtype=jnp.int32)
    row_positions = row_start + jnp.arange(query_rows, dtype=jnp.int32)
    query_offset = ffn_index * query_cols
    key_offset = ffn_index * key_cols
    score_scale = 1.0 / math.sqrt(HEAD_DIM)
    down_flattened = adapter_down.reshape(3 * ADAPTER_RANK, adapter_down.shape[2])
    paired = ffn_count > KV_HEADS
    parity = ffn_index % 2
    rank_terms = contract_last(hidden_rows_full, down_flattened)
    upstream_terms = contract_last(upstream_gradient_full, output_up)
    rank_sum, upstream_sum = lax.psum((rank_terms, upstream_terms), "width")
    reduced_hidden = rank_sum.astype(jnp.bfloat16)
    output_reduced = upstream_sum.astype(jnp.bfloat16)
    low_rows = lax.dynamic_slice_in_dim(reduced_hidden, row_start, query_rows, 0)
    output_token_rows = lax.dynamic_slice_in_dim(output_reduced, row_start, query_rows, 0)
    query_part = jnp.dot(hidden_rows_full, query_frozen_weight, preferred_element_type=jnp.float32)
    query_gradient_summed = lax.psum_scatter(
        query_part.astype(jnp.bfloat16), "width", scatter_dimension=0, tiled=True
    ).astype(jnp.float32)
    query_projected = query_gradient_summed + adapter_scale * jnp.dot(
        low_rows[:, :ADAPTER_RANK], query_up_map, preferred_element_type=jnp.float32
    )
    query_states = rotate(query_projected, row_positions, query_offset, 1.0).astype(jnp.bfloat16)
    key_part = jnp.dot(
        hidden_rows_full, key_value_frozen_weight[0], preferred_element_type=jnp.float32
    )
    value_part = jnp.dot(
        hidden_rows_full, key_value_frozen_weight[1], preferred_element_type=jnp.float32
    )
    key_gradient_summed, value_gradient_summed = (
        lax.psum_scatter(
            key_part.astype(jnp.bfloat16), "width", scatter_dimension=0, tiled=True
        ).astype(jnp.float32),
        lax.psum_scatter(
            value_part.astype(jnp.bfloat16), "width", scatter_dimension=0, tiled=True
        ).astype(jnp.float32),
    )
    key_projected = key_gradient_summed + adapter_scale * jnp.dot(
        low_rows[:, ADAPTER_RANK : 2 * ADAPTER_RANK],
        key_value_up_maps[0],
        preferred_element_type=jnp.float32,
    )
    value_projected = value_gradient_summed + adapter_scale * jnp.dot(
        low_rows[:, 2 * ADAPTER_RANK :], key_value_up_maps[1], preferred_element_type=jnp.float32
    )
    key_block = rotate(key_projected, row_positions, key_offset, 1.0).astype(jnp.bfloat16)
    value_block = value_projected.astype(jnp.bfloat16)
    key_states, value_state_rows = (
        lax.all_gather(key_block, "width", axis=0, tiled=True),
        lax.all_gather(value_block, "width", axis=0, tiled=True),
    )
    if paired:
        other_key, other_value = from_partner((key_states, value_state_rows), "ffn", 0)
        key_states = jnp.where(
            parity == 0,
            jnp.concatenate([key_states, other_key], 1),
            jnp.concatenate([other_key, key_states], 1),
        )
        value_state_rows = jnp.where(
            parity == 0,
            jnp.concatenate([value_state_rows, other_value], 1),
            jnp.concatenate([other_value, value_state_rows], 1),
        )
    local_heads = query_cols // HEAD_DIM
    local_groups = key_states.shape[1] // HEAD_DIM
    group_size = local_heads // local_groups
    query_four = query_states.reshape(query_rows, local_groups, group_size, HEAD_DIM)
    key_three = key_states.reshape(token_count, local_groups, HEAD_DIM)
    value_three = value_state_rows.reshape(token_count, local_groups, HEAD_DIM)
    causal = row_positions[:, None] >= positions[None, :]
    scores = (
        jnp.einsum("qkgd,skd->kgqs", query_four, key_three, preferred_element_type=jnp.float32)
        * score_scale
    )
    scores = jnp.where(causal[None, None, :, :], scores, -jnp.inf)
    shifted = jnp.exp(scores - jnp.max(scores, axis=-1, keepdims=True))
    probs = shifted / jnp.sum(shifted, axis=-1, keepdims=True)
    prob_weights = probs.astype(jnp.bfloat16)
    attention_four = jnp.einsum(
        "kgqs,skd->qkgd", prob_weights, value_three, preferred_element_type=jnp.float32
    ).astype(jnp.bfloat16)
    attention_output = attention_four.reshape(query_rows, query_cols)
    out_part = contract_last(upstream_gradient_full, output_frozen_weight)
    output_gradient_summed = lax.psum_scatter(
        out_part.astype(jnp.bfloat16), "width", scatter_dimension=0, tiled=True
    ).astype(jnp.float32)
    attention_output_gradient = (
        output_gradient_summed
        + adapter_scale
        * jnp.dot(output_token_rows, output_down_map, preferred_element_type=jnp.float32)
    ).astype(jnp.bfloat16)
    grad_four = attention_output_gradient.reshape(query_rows, local_groups, group_size, HEAD_DIM)
    prob_grad = jnp.einsum(
        "qkgd,skd->kgqs", grad_four, value_three, preferred_element_type=jnp.float32
    )
    delta = jnp.einsum(
        "qkgd,qkgd->kgq", grad_four, attention_four, preferred_element_type=jnp.float32
    )
    score_grad = (probs * (prob_grad - delta[:, :, :, None]) * score_scale).astype(jnp.bfloat16)
    query_rot_grad = jnp.einsum(
        "kgqs,skd->qkgd", score_grad, key_three, preferred_element_type=jnp.float32
    ).reshape(query_rows, query_cols)
    key_part_grad = jnp.einsum(
        "kgqs,qkgd->skd", score_grad, query_four, preferred_element_type=jnp.float32
    ).reshape(token_count, local_groups * HEAD_DIM)
    value_part_grad = jnp.einsum(
        "kgqs,qkgd->skd", prob_weights, grad_four, preferred_element_type=jnp.float32
    ).reshape(token_count, local_groups * HEAD_DIM)
    query_block_grad = rotate(query_rot_grad, row_positions, query_offset, -1.0).astype(
        jnp.bfloat16
    )

    def own_half(values):
        return lax.dynamic_slice_in_dim(values, parity * key_cols, key_cols, 1)

    def other_half(values):
        return lax.dynamic_slice_in_dim(values, (1 - parity) * key_cols, key_cols, 1)

    key_total, value_total = lax.psum((key_part_grad, value_part_grad), "width")
    if paired:
        sent_key, sent_value = from_partner(
            (other_half(key_total), other_half(value_total)), "ffn", 0
        )
        key_total = own_half(key_total) + sent_key
        value_total = own_half(value_total) + sent_value
    key_rows_gradient = rotate(key_total, positions, key_offset, -1.0).astype(jnp.bfloat16)
    value_rows_gradient = value_total.astype(jnp.bfloat16)
    query_rows_gradient = lax.all_gather(query_block_grad, "width", axis=0, tiled=True)
    input_part = (
        contract_last(query_rows_gradient, query_frozen_weight)
        + contract_last(key_rows_gradient, key_value_frozen_weight[0])
        + contract_last(value_rows_gradient, key_value_frozen_weight[1])
    )
    rank_grad_terms = jnp.concatenate(
        [
            contract_last(query_rows_gradient, query_up_map),
            contract_last(key_rows_gradient, key_value_up_maps[0]),
            contract_last(value_rows_gradient, key_value_up_maps[1]),
        ],
        axis=1,
    )
    rank_gradient = lax.psum(rank_grad_terms, "ffn").astype(jnp.bfloat16)
    input_sum = lax.psum_scatter(
        input_part.astype(jnp.bfloat16), "ffn", scatter_dimension=0, tiled=True
    ).astype(jnp.float32)
    own_rows = token_count // ffn_count
    rank_gradient_token_rows = lax.dynamic_slice_in_dim(
        rank_gradient, ffn_index * own_rows, own_rows, 0
    )
    hidden_gradient = (
        input_sum
        + adapter_scale
        * jnp.dot(rank_gradient_token_rows, down_flattened, preferred_element_type=jnp.float32)
    ).astype(jnp.bfloat16)
    down_map_gradient = (adapter_scale * contract_leading(rank_gradient, hidden_rows_full)).reshape(
        adapter_down.shape
    )
    query_up_map_gradient = adapter_scale * contract_leading(
        reduced_hidden[:, :ADAPTER_RANK], query_rows_gradient
    )
    key_value_up_maps_gradient = adapter_scale * jnp.stack(
        [
            contract_leading(reduced_hidden[:, ADAPTER_RANK : 2 * ADAPTER_RANK], key_rows_gradient),
            contract_leading(reduced_hidden[:, 2 * ADAPTER_RANK :], value_rows_gradient),
        ]
    )
    outer_terms = contract_last(attention_output, output_down_map)
    outer_rows = lax.psum(outer_terms, "ffn").astype(jnp.bfloat16)
    outer_product_rank = lax.all_gather(outer_rows, "width", axis=0, tiled=True)
    output_down_map_gradient = adapter_scale * lax.psum(
        contract_leading(output_token_rows, attention_output), "width"
    )
    output_up_map_gradient = adapter_scale * contract_leading(
        outer_product_rank, upstream_gradient_full
    )
    return (
        hidden_gradient,
        down_map_gradient,
        query_up_map_gradient,
        key_value_up_maps_gradient,
        output_down_map_gradient,
        output_up_map_gradient,
    )


def solution(mesh):
    placed = (
        P(("groups", "ffn"), "width"),
        P(("groups", "ffn"), "width"),
        P("width", "ffn"),
        P(None, "width", "ffn"),
        P("ffn", "width"),
        P("groups", None, "width"),
        P("groups", "ffn"),
        P("groups", None, "ffn"),
        P("groups", "ffn"),
        P("groups", "width"),
    )
    return jax.shard_map(
        shards,
        mesh=mesh,
        in_specs=placed,
        out_specs=(
            P(("groups", "ffn"), "width"),
            P("groups", None, "width"),
            P("groups", "ffn"),
            P("groups", None, "ffn"),
            P("groups", "ffn"),
            P("groups", "width"),
        ),
        check_vma=False,
    )
```

profile of v0, /device:TPU:0, one launch (start us, length us, event | category | flops | bytes accessed | tf_op | source)
XLA Modules:
  0.0 590.3 jit_solution(5935523858000634703)
XLA Ops:
  8.7 38.0 %all-gather.4.cloned.1.call-done = bf16[1024,2048]{1,0:T(8,128)(2,1)} async-done(((bf16[256,2048]{1,0:T(8,128)(2,1)}), bf16[1024,2048]{1,0:T(8,128)(2,1)}) %all-gather.4.cloned.1.call-update) | async-done | bytes 4194320 | tf_op jit(solution)/shard_map/all_gather | solution.py:63
  55.7 14.6 %convolution_convert_fusion.1 = bf16[1024,2048]{1,0:T(8,128)(2,1)} fusion(bf16[1024,2048]{1,0:T(8,128)(2,1)} %all-gather.4.cloned.1.call-done, bf16[2048,2048]{1,0:T(8,128)(2,1)} %param.12), kind=kOutput, calls=%fused_computation.15 | convolution fusion | flops 8592031744 | bytes 16777216 | tf_op jit(solution)/shard_map/dot_general | solution.py:86
  70.4 12.4 %all-gather.6.cloned.1.call-done = bf16[1024,2048]{1,0:T(8,128)(2,1)} async-done(((bf16[256,2048]{1,0:T(8,128)(2,1)}), bf16[1024,2048]{1,0:T(8,128)(2,1)}) %all-gather.6.cloned.1.call-update) | async-done | bytes 4194320 | tf_op jit(solution)/shard_map/all_gather | solution.py:64
  82.8 13.9 %convolution_convert_fusion = bf16[1024,2048]{1,0:T(8,128)(2,1)} fusion(bf16[1024,2048]{1,0:T(8,128)(2,1)} %all-gather.6.cloned.1.call-done, bf16[2048,2048]{1,0:T(8,128)(2,1)} %param.14), kind=kOutput, calls=%fused_computation.14 | convolution fusion | flops 8592031744 | bytes 16777216 | tf_op jit(solution)/shard_map/dot_general | solution.py:35
  103.0 27.6 %all-reduce.9 = (bf16[1024,48]{0,1:T(8,128)(2,1)S(1)}, bf16[1024,16]{0,1:T(8,128)(2,1)S(1)}) all-reduce(f32[1024,48]{0,1:T(8,128)S(1)} %fusion.109, f32[1024,16]{0,1:T(8,128)S(1)} %fusion.110), channel_id=1, replica_groups=mesh['groups'=2,'ffn'=4,'width'=4] {'width'}, use_global_device_ids=true, to_apply=%region_1.0 | all-reduce | flops 65536 | bytes 393216 | tf_op jit(solution)/shard_map/psum | solution.py:81
  133.3 19.4 %all_gather.19 = bf16[1024,256]{1,0:T(8,128)(2,1)S(1)} all-gather(bf16[256,256]{1,0:T(8,128)(2,1)S(1)} %fusion.57), channel_id=1, replica_groups=mesh['groups'=2,'ffn'=4,'width'=4] {'width'}, dimensions={0}, use_global_device_ids=true | all-gather | bytes 655360 | tf_op jit(solution)/shard_map/all_gather | solution.py:119
  155.1 19.7 %all_gather.20 = bf16[1024,256]{1,0:T(8,128)(2,1)S(1)} all-gather(bf16[256,256]{1,0:T(8,128)(2,1)S(1)} %fusion.30), channel_id=1, replica_groups=mesh['groups'=2,'ffn'=4,'width'=4] {'width'}, dimensions={0}, use_global_device_ids=true | all-gather | bytes 655360 | tf_op jit(solution)/shard_map/all_gather | solution.py:120
  176.1 44.6 %reduce-scatter.8.cloned.1.call-done = bf16[256,2048]{1,0:T(8,128)(2,1)} async-done(((bf16[1024,2048]{1,0:T(8,128)(2,1)}), bf16[256,2048]{1,0:T(8,128)(2,1)}) %reduce-scatter.8.cloned.1.call-update) | async-done | bytes 1048592 | tf_op jit(solution)/shard_map/reduce_scatter | solution.py:87
  223.3 8.7 %fusion.43 = bf16[32,8,16,128]{3,1,2,0:T(8,128)(2,1)S(1)} fusion(f32[256,2047]{1,0:T(8,128)S(1)} %get-tuple-element.17, f32[256,1]{1,0:T(8,128)S(1)} %get-tuple-element.19, f32[256,1]{1,0:T(8,128)S(1)} %get-tuple-element.18, f32[256,2047]{1,0:T(8,128)S(1)} %get-tuple-element.16, pred[2048]{0:T(1024)(128)(4,1)S(1)} %fusion.82, f32[256,2048]{1,0:T(8,128)S(1)} %fusion.15, ...), kind=kLoop, calls=%fused_computation.72 | loop fusion | flops 4718592 | bytes 7351296
  233.2 66.6 %reduce-scatter.12.cloned.1.call-done = bf16[256,2048]{1,0:T(8,128)(2,1)} async-done(((bf16[1024,2048]{1,0:T(8,128)(2,1)}), bf16[256,2048]{1,0:T(8,128)(2,1)}) %reduce-scatter.12.cloned.1.call-update) | async-done | bytes 1048592 | tf_op jit(solution)/shard_map/reduce_scatter | solution.py:154
  303.7 12.4 %fusion.104 = (f32[2,8,256]{2,1,0:T(8,128)S(1)}, f32[2,8,256,1024]{2,3,1,0:T(8,128)}) fusion(pred[256,1024]{0,1:T(8,128)(4,1)} %iota_compare_fusion, bf16[1024,2,128,1]{0,2,3,1:T(8,128)(2,1)} %copy.41, bf16[256,2,8,128]{3,2,1,0:T(8,128)(2,1)} %bitcast.131), kind=kOutput, calls=%fused_computation.153 | convolution fusion | flops 1090520064 | bytes 18628608 | tf_op jit(solution)/shard_map/sub | solution.py:146
  316.2 7.5 %fusion.8 = bf16[2,8,256,1024]{2,3,1,0:T(8,128)(2,1)S(1)} fusion(f32[2,8,256,1024]{2,3,1,0:T(8,128)} %get-tuple-element.29, f32[2,8,256]{2,1,0:T(8,128)S(1)} %get-tuple-element.28), kind=kLoop, calls=%fused_computation.13 | loop fusion | flops 8388608 | bytes 25182208 | tf_op jit(solution)/shard_map/convert_element_type | solution.py:148
  331.0 7.2 %fusion.3 = bf16[2,8,256,1024]{2,3,1,0:T(8,128)(2,1)} fusion(f32[2,8,256]{2,1,0:T(8,128)S(1)} %get-tuple-element.30, f32[2,8,256,1024]{2,3,1,0:T(8,128)S(1)} %bitcast.123, f32[2,8,256]{2,1,0:T(8,128)S(1)} %get-tuple-element.28, bf16[1024,2,128,1]{0,2,3,1:T(8,128)(2,1)} %copy.33, bf16[256,2,8,128]{3,2,1,0:T(8,128)(2,1)S(1)} %bitcast.125), kind=kOutput, calls=%fused_computation.4 | convolution fusion | flops 1094713344 | bytes 26771456 | tf_op jit(solution)/shard_map/qkgd,skd->kgqs/dot_general | solution.py:163
  338.2 12.4 %copy.44 = bf16[2,8,256,1024]{3,1,0,2:T(8,128)(2,1)} copy(bf16[2,8,256,1024]{2,3,1,0:T(8,128)(2,1)} %fusion.3) | data formatting | bytes 16777216 | tf_op jit(solution)/shard_map/convert_element_type | solution.py:169
  350.6 6.1 %fusion.111 = f32[2,128,8,256]{3,1,2,0:T(8,128)} fusion(bf16[1024,2,128,1]{0,2,3,1:T(8,128)(2,1)S(1)} %copy-done.16, bf16[2,8,256,1024]{2,3,1,0:T(8,128)(2,1)} %fusion.3), kind=kOutput, calls=%fused_computation.156 | convolution fusion | flops 1073741824 | bytes 11010048 | tf_op jit(solution)/shard_map/kgqs,skd->qkgd/dot_general | solution.py:170
  363.5 9.3 %fusion.21 = bf16[256,2048]{1,0:T(8,128)(2,1)} fusion(f32[256,2048]{1,0:T(8,128)S(1)} %copy.55, f32[256,1]{1,0:T(8,128)S(1)} %get-tuple-element.13, f32[256,2047]{1,0:T(8,128)S(1)} %get-tuple-element.15, f32[256,2047]{1,0:T(8,128)S(1)} %get-tuple-element.14, f32[256,1]{1,0:T(8,128)S(1)} %get-tuple-element.12, f32[2048]{0:T(1024)S(1)} %multiply_exponential_fusion, ...), kind=kLoop, calls=%fused_computation.36 | loop fusion | flops 5242880 | bytes 7351296 | tf_op jit(solution)/shard_map/convert_element_type | solution.py:179
  372.8 12.4 %copy.46 = bf16[2,8,256,1024]{3,1,0,2:T(8,128)(2,1)} copy(bf16[2,8,256,1024]{2,3,1,0:T(8,128)(2,1)} %copy-done.1) | data formatting | bytes 16777216 | tf_op jit(solution)/shard_map/convert_element_type | solution.py:148
  385.3 4.8 fusion.114
  390.0 60.6 %all-reduce.10 = bf16[1024,256]{0,1:T(8,128)(2,1)S(1)} all-reduce(f32[1024,256]{0,1:T(8,128)S(1)} %bitcast.133), channel_id=1, replica_groups=mesh['groups'=2,'ffn'=4,'width'=4] {'width'}, use_global_device_ids=true, to_apply=%region_9.10 | all-reduce | flops 262144 | bytes 1572864 | tf_op jit(solution)/shard_map/psum | solution.py:189
  453.4 4.8 fusion.33
  462.9 55.6 %all-gather.8.cloned.1.call-done = bf16[1024,2048]{1,0:T(8,128)(2,1)} async-done(((bf16[256,2048]{1,0:T(8,128)(2,1)}), bf16[1024,2048]{1,0:T(8,128)(2,1)}) %all-gather.8.cloned.1.call-update) | async-done | bytes 4194320 | tf_op jit(solution)/shard_map/all_gather | solution.py:198
  518.4 12.7 %fusion.112 = f32[1024,2048]{1,0:T(8,128)S(1)} fusion(bf16[1024,2048]{1,0:T(8,128)(2,1)} %all-gather.8.cloned.1.call-done, bf16[2048,2048]{1,0:T(8,128)(2,1)} %param.12), kind=kOutput, calls=%fused_computation.157 | convolution fusion | flops 8589934592 | bytes 20971520 | tf_op jit(solution)/shard_map/dot_general | solution.py:35
  542.4 17.8 %all-reduce.11 = (bf16[1024,48]{0,1:T(8,128)(2,1)S(1)}, bf16[256,16]{1,0:T(8,128)(2,1)S(1)}) all-reduce(f32[1024,48]{0,1:T(8,128)S(1)} %pad_maximum_fusion, f32[256,16]{1,0:T(8,128)S(1)} %fusion.116), channel_id=1, replica_groups=mesh['groups'=2,'ffn'=4,'width'=4] {'ffn'}, use_global_device_ids=true, to_apply=%region_11.12 | all-reduce | flops 53248 | bytes 319488 | tf_op jit(solution)/shard_map/psum | solution.py:212
  560.2 13.9 %all_gather.23 = bf16[1024,16]{1,0:T(8,128)(2,1)S(1)} all-gather(bf16[256,16]{1,0:T(8,128)(2,1)S(1)} %get-tuple-element.11), channel_id=1, replica_groups=mesh['groups'=2,'ffn'=4,'width'=4] {'width'}, dimensions={0}, use_global_device_ids=true | all-gather | bytes 40960 | tf_op jit(solution)/shard_map/all_gather | solution.py:239
  (131 shorter events, 72.3 us)
Async XLA Ops:
  7.2 90.7 %copy-start = (bf16[3,16,2048]{2,1,0:T(8,128)(2,1)S(1)}, bf16[3,16,2048]{2,1,0:T(8,128)(2,1)}, u32[]{:S(2)}) copy-start(bf16[3,16,2048]{2,1,0:T(8,128)(2,1)} %param.15) | copy-start | bytes 589828
  7.2 39.6 %all-gather.4.cloned.1.call-start = ((), (), s32[]{:S(2)}) async-start(), calls=%async_computation.5 | async-start | bytes 5242880 | tf_op jit(solution)/shard_map/all_gather | solution.py:63
  7.9 74.9 %all-gather.6.cloned.1.call-start = ((), (), s32[]{:S(2)}) async-start(), calls=%async_computation.9 | async-start | bytes 5242880 | tf_op jit(solution)/shard_map/all_gather | solution.py:64
  8.7 42.7 %copy-start.12 = (bf16[2,2048,256]{2,1,0:T(8,128)(2,1)S(1)}, bf16[2,2048,256]{2,1,0:T(8,128)(2,1)}, u32[]{:S(2)}) copy-start(bf16[2,2048,256]{2,1,0:T(8,128)(2,1)} %param.13) | copy-start | bytes 6291460
  8.7 122.0 %reduce-scatter.6.cloned.1.call-start = ((), (), s32[]{:S(2)}) async-start(), calls=%async_computation.6 | async-start | bytes 655360 | tf_op jit(solution)/shard_map/reduce_scatter | solution.py:101
  51.3 102.7 %reduce-scatter.10.cloned.1.call-start = ((), (), s32[]{:S(2)}) async-start(), calls=%async_computation.8 | async-start | bytes 655360 | tf_op jit(solution)/shard_map/reduce_scatter | solution.py:104
  55.6 165.1 %reduce-scatter.8.cloned.1.call-start = ((), (), s32[]{:S(2)}) async-start(), calls=%async_computation.7 | async-start | bytes 5242880 | tf_op jit(solution)/shard_map/reduce_scatter | solution.py:87
  70.3 229.5 %reduce-scatter.12.cloned.1.call-start = ((), (), s32[]{:S(2)}) async-start(), calls=%async_computation.10 | async-start | bytes 5242880 | tf_op jit(solution)/shard_map/reduce_scatter | solution.py:154
  96.8 353.9 %all-reduce.8.cloned.1.call-start = ((), (), s32[]{:S(2)}) async-start(), calls=%async_computation.13 | async-start | bytes 2359296 | tf_op jit(solution)/shard_map/psum | solution.py:189
  101.8 28.9 %copy-start.23 = (bf16[2,16,256]{2,1,0:T(8,128)(2,1)S(1)}, bf16[2,16,256]{2,1,0:T(8,128)(2,1)}, u32[]{:S(2)}) copy-start(bf16[2,16,256]{2,1,0:T(8,128)(2,1)} %param.17) | copy-start | bytes 49156
  130.7 90.1 %copy-start.19 = (bf16[1024,48]{0,1:T(8,128)(2,1)}, bf16[1024,48]{0,1:T(8,128)(2,1)S(1)}, u32[]{:S(2)}) copy-start(bf16[1024,48]{0,1:T(8,128)(2,1)S(1)} %get-tuple-element.6) | copy-start | bytes 294916
  131.9 88.9 %copy-start.17 = (bf16[16,2048]{1,0:T(8,128)(2,1)S(1)}, bf16[16,2048]{1,0:T(8,128)(2,1)}, u32[]{:S(2)}) copy-start(bf16[16,2048]{1,0:T(8,128)(2,1)} %param.16) | copy-start | bytes 196612
  223.3 76.5 %copy-start.18 = (bf16[16,2048]{1,0:T(8,128)(2,1)S(1)}, bf16[16,2048]{1,0:T(8,128)(2,1)}, u32[]{:S(2)}) copy-start(bf16[16,2048]{1,0:T(8,128)(2,1)} %param.18) | copy-start | bytes 196612
  316.2 7.5 %copy-start.15 = (bf16[1024,2,128,1]{0,2,3,1:T(8,128)(2,1)S(1)}, bf16[1024,2,128,1]{0,2,3,1:T(8,128)(2,1)}, u32[]{:S(2)}) copy-start(bf16[1024,2,128,1]{0,2,3,1:T(8,128)(2,1)} %copy.33) | copy-start | bytes 1572868
  316.2 11.8 %slice-start = ((s8[16777216]{0:T(1024)(128)(4,1)}), s8[4194304]{0:T(1024)(128)(4,1)S(1)}, s32[]{:S(2)}) async-start(s8[16777216]{0:T(1024)(128)(4,1)} %bitcast.122), calls=%async_computation.14 | async-start | bytes 8388608
  316.2 11.8 %slice-start.1 = ((s8[16777216]{0:T(1024)(128)(4,1)}), s8[4194304]{0:T(1024)(128)(4,1)S(1)}, s32[]{:S(2)}) async-start(s8[16777216]{0:T(1024)(128)(4,1)} %bitcast.122), calls=%async_computation.15 | async-start | bytes 8388608
  316.2 13.6 %slice-start.2 = ((s8[16777216]{0:T(1024)(128)(4,1)}), s8[4194304]{0:T(1024)(128)(4,1)S(1)}, s32[]{:S(2)}) async-start(s8[16777216]{0:T(1024)(128)(4,1)} %bitcast.122), calls=%async_computation.16 | async-start | bytes 8388608
  328.0 31.6 %copy-start.8 = (bf16[2,128,8,256]{3,1,2,0:T(8,128)(2,1)}, bf16[2,128,8,256]{3,1,2,0:T(8,128)(2,1)S(1)}, u32[]{:S(2)}) copy-start(bf16[2,128,8,256]{3,1,2,0:T(8,128)(2,1)S(1)} %get-tuple-element.31) | copy-start | bytes 3145732
  338.2 12.4 %copy-start.16 = (bf16[1024,2,128,1]{0,2,3,1:T(8,128)(2,1)S(1)}, bf16[1024,2,128,1]{0,2,3,1:T(8,128)(2,1)}, u32[]{:S(2)}) copy-start(bf16[1024,2,128,1]{0,2,3,1:T(8,128)(2,1)} %copy.41) | copy-start | bytes 1572868
  362.6 155.8 %all-gather.8.cloned.1.call-start = ((), (), s32[]{:S(2)}) async-start(), calls=%async_computation.11 | async-start | bytes 5242880 | tf_op jit(solution)/shard_map/all_gather | solution.py:198
  372.8 207.9 %reduce-scatter.14.cloned.1.call-start = ((), (), s32[]{:S(2)}) async-start(), calls=%async_computation.12 | async-start | bytes 5242880 | tf_op jit(solution)/shard_map/reduce_scatter | solution.py:213
  518.4 12.7 %copy-start.2 = (f32[1024,2048]{1,0:T(8,128)S(1)}, f32[1024,2048]{1,0:T(8,128)}, u32[]{:S(2)}) copy-start(f32[1024,2048]{1,0:T(8,128)} %fusion.39) | copy-start | bytes 25165828
  518.4 12.7 %copy-start.14 = (bf16[2,2048,256]{2,1,0:T(8,128)(2,1)S(1)}, bf16[2,2048,256]{2,1,0:T(8,128)(2,1)}, u32[]{:S(2)}) copy-start(bf16[2,2048,256]{2,1,0:T(8,128)(2,1)} %param.13) | copy-start | bytes 6291460
  560.1 17.6 %copy-start.6 = (bf16[1024,2048]{1,0:T(8,128)(2,1)S(1)}, bf16[1024,2048]{1,0:T(8,128)(2,1)}, u32[]{:S(2)}) copy-start(bf16[1024,2048]{1,0:T(8,128)(2,1)} %all-gather.6.cloned.1.call-done) | copy-start | bytes 12582916
  (13 other events, 63.2 us)
Sparse Core Ops, SparseCore 0:
  9.5 37.1 all-gather.3
  48.3 34.4 all-gather.5
  85.7 21.8 reduce-scatter.5
  109.7 21.9 reduce-scatter.9
  133.8 86.8 reduce-scatter.7
  222.9 76.8 reduce-scatter.11
  362.7 73.6 all-reduce.7
  438.5 79.8 all-gather.7
  534.7 45.0 reduce-scatter.13
where the time goes:
time: 599 us; the launch traced here: 590 us
  waiting for transfers between devices  219 us (37%)
  blocking collectives  159 us (27%)
  matrix products  118 us (20%)
  local copies, waits for them, and re-layouts  44.9 us (7%)
  other arithmetic  34 us (6%)
  between operations  14.8 us (2%)
    reduce_scatter x1, waiting for transfers between devices, shards(): lax.psum_scatter(out_part.astype(jnp.bfloat16), 'width', scatter_dimensio...  66.6 us
    psum x1, blocking collectives, shards(): key_total, value_total = lax.psum((key_part_grad, value_part_grad), 'width')  60.6 us
    all_gather x1, waiting for transfers between devices, shards(): lax.all_gather(query_block_grad, 'width', axis=0, tiled=True)  55.6 us
    reduce_scatter x1, waiting for transfers between devices, shards(): lax.psum_scatter(query_part.astype(jnp.bfloat16), 'width', scatter_dimens...  44.6 us
    dot_general x10, matrix products, contract_last(): lax.dot_general(left_side, right_side, (((1,), (1,)), ((), ())), preferre...  44.5 us
    all_gather x1, waiting for transfers between devices, shards(): lax.all_gather(hidden, 'ffn', axis=0, tiled=True)  38 us
    psum x1, blocking collectives, shards(): rank_sum, upstream_sum = lax.psum((rank_terms, upstream_terms), 'width')  27.6 us
    all_gather x1, blocking collectives, shards(): lax.all_gather(value_block, 'width', axis=0, tiled=True)  19.7 us
  transfers between devices with their start and end apart: 9, of which 5 were waited for; matrix products, arithmetic and copies ran while one was open for 19% of the time, Pallas kernels for 0%

commit v1 on v0

--- a/solution.py
+++ b/solution.py
@@ -1,13 +1,19 @@
+import functools
 import math
 
 import jax
 import jax.numpy as jnp
 from jax import lax
+from jax.experimental import pallas as pl
+from jax.experimental.pallas import tpu as pltpu
 from jax.sharding import PartitionSpec as P
 
 KV_HEADS = 8
 HEAD_DIM = 128
 ADAPTER_RANK = 16
+BLOCKS = 4
+CHUNK_HEADS = 2
+PIECES = 2
 
 
 adapter_scale = 2.0
@@ -253,6 +259,325 @@
     )
 
 
+def causal_heads(scale, own_q, add_q, low, up, own_g, add_g, low_g, up_g, key, value, cosine, sine,
+                 attention, query_grad, key_grad, value_grad):
+    rows, columns = own_q.shape
+    block = rows // BLOCKS
+    even = lax.broadcasted_iota(jnp.int32, (rows, HEAD_DIM), 1) % 2 == 0
+    key_all = key[...]
+    value_all = value[...]
+    dims_last = (((1,), (1,)), ((), ()))
+    dims_first = (((0,), (0,)), ((), ()))
+
+    def turned(values, direction):
+        following = pltpu.roll(values, HEAD_DIM - 1, 1)
+        preceding = pltpu.roll(values, 1, 1)
+        partner = jnp.where(even, -following, preceding)
+        return values * cosine[...] + direction * partner * sine[...]
+
+    key_grad[...] = jnp.zeros_like(key_grad)
+    value_grad[...] = jnp.zeros_like(value_grad)
+    for head in range(columns // HEAD_DIM):
+        cols = slice(head * HEAD_DIM, (head + 1) * HEAD_DIM)
+        query_sum = own_q[:, cols].astype(jnp.float32) + add_q[:, cols].astype(jnp.float32)
+        query_sum += adapter_scale * jnp.dot(
+            low[...], up[:, cols], preferred_element_type=jnp.float32
+        )
+        query = turned(query_sum, 1.0).astype(jnp.bfloat16)
+        grad_sum = own_g[:, cols].astype(jnp.float32) + add_g[:, cols].astype(jnp.float32)
+        grad_sum += adapter_scale * jnp.dot(
+            low_g[...], up_g[:, cols], preferred_element_type=jnp.float32
+        )
+        grad = grad_sum.astype(jnp.bfloat16)
+        query_terms = []
+        for index in range(BLOCKS):
+            start, stop = index * block, (index + 1) * block
+            query_block = query[start:stop]
+            grad_block = grad[start:stop]
+            key_part = key_all[:stop]
+            value_part = value_all[:stop]
+            scores = (
+                lax.dot_general(query_block, key_part, dims_last, preferred_element_type=jnp.float32)
+                * scale
+            )
+            row = start + lax.broadcasted_iota(jnp.int32, (block, stop), 0)
+            column = lax.broadcasted_iota(jnp.int32, (block, stop), 1)
+            scores = jnp.where(row >= column, scores, -jnp.inf)
+            shifted = jnp.exp(scores - jnp.max(scores, axis=1, keepdims=True))
+            probs = shifted * (1.0 / jnp.sum(shifted, axis=1, keepdims=True))
+            weights = probs.astype(jnp.bfloat16)
+            attended = jnp.dot(weights, value_part, preferred_element_type=jnp.float32).astype(
+                jnp.bfloat16
+            )
+            attention[start:stop, cols] = attended
+            prob_grad = lax.dot_general(
+                grad_block, value_part, dims_last, preferred_element_type=jnp.float32
+            )
+            delta = jnp.sum(
+                grad_block.astype(jnp.float32) * attended.astype(jnp.float32), axis=1, keepdims=True
+            )
+            score_grad = (probs * ((prob_grad - delta) * scale)).astype(jnp.bfloat16)
+            query_terms.append(jnp.dot(score_grad, key_part, preferred_element_type=jnp.float32))
+            key_grad[:stop, :] += lax.dot_general(
+                score_grad, query_block, dims_first, preferred_element_type=jnp.float32
+            )
+            value_grad[:stop, :] += lax.dot_general(
+                weights, grad_block, dims_first, preferred_element_type=jnp.float32
+            )
+        query_grad[:, cols] = turned(jnp.concatenate(query_terms, 0), -1.0).astype(jnp.bfloat16)
+
+
+def attend(scale, *operands):
+    rows, columns = operands[0].shape
+    pairs = rows * rows * columns
+    return pl.pallas_call(
+        functools.partial(causal_heads, scale),
+        out_shape=(
+            jax.ShapeDtypeStruct((rows, columns), jnp.bfloat16),
+            jax.ShapeDtypeStruct((rows, columns), jnp.bfloat16),
+            jax.ShapeDtypeStruct((rows, HEAD_DIM), jnp.float32),
+            jax.ShapeDtypeStruct((rows, HEAD_DIM), jnp.float32),
+        ),
+        in_specs=[pl.BlockSpec(memory_space=pltpu.VMEM)] * len(operands),
+        out_specs=(pl.BlockSpec(memory_space=pltpu.VMEM),) * 4,
+        compiler_params=pltpu.CompilerParams(vmem_limit_bytes=40 * 1024 * 1024),
+        cost_estimate=pl.CostEstimate(
+            flops=12 * pairs, bytes_accessed=16 * rows * columns, transcendentals=pairs // HEAD_DIM
+        ),
+    )(*operands)
+
+
+def gather_tokens(block, axis):
+    count = lax.axis_size(axis)
+    index = lax.axis_index(axis)
+    held = block
+    for bit in reversed(range(count.bit_length() - 1)):
+        other = from_partner(held, axis, bit)
+        low_side = (index >> bit) % 2 == 0
+        held = jnp.stack([jnp.where(low_side, held, other), jnp.where(low_side, other, held)])
+    bits = count.bit_length() - 1
+    order = tuple(reversed(range(bits))) + (bits, bits + 1)
+    return held.transpose(order).reshape(count * block.shape[0], block.shape[1])
+
+
+def scatter_tokens(parts, axis):
+    count = lax.axis_size(axis)
+    index = lax.axis_index(axis)
+    bits = count.bit_length() - 1
+    rows = parts.shape[0] // count
+    held = parts.reshape((2,) * bits + (rows, parts.shape[1]))
+    for bit in range(bits):
+        dim = bits - 1 - bit
+        side = (index >> bit) % 2
+        mine = lax.dynamic_index_in_dim(held, side, dim, keepdims=False)
+        theirs = lax.dynamic_index_in_dim(held, 1 - side, dim, keepdims=False)
+        received = from_partner(theirs.astype(jnp.bfloat16), axis, bit)
+        held = mine.astype(jnp.float32) + received.astype(jnp.float32)
+    return held
+
+
+def end_streams(
+    hidden,
+    upstream,
+    query_frozen_weight,
+    key_value_frozen_weight,
+    output_frozen_weight,
+    adapter_down,
+    query_up_map,
+    key_value_up_maps,
+    output_down_map,
+    output_up,
+):
+    ffn_count = lax.axis_size("ffn")
+    width_count = lax.axis_size("width")
+    ffn_index = lax.axis_index("ffn")
+    width_index = lax.axis_index("width")
+    last = width_count - 1
+    hops = [
+        [(hop, hop + 1), (last - hop, last - hop - 1)] for hop in range(last)
+    ]
+    is_last = width_index == last
+    is_end = (width_index == 0) | is_last
+    hidden_full = gather_tokens(hidden, "ffn")
+    upstream_full = gather_tokens(upstream, "ffn")
+    token_count = hidden_full.shape[0]
+    query_cols = query_frozen_weight.shape[1]
+    group_cols = query_cols // 2
+    chunks = group_cols // (HEAD_DIM * CHUNK_HEADS)
+    chunk_cols = group_cols // chunks
+    positions = jnp.arange(token_count, dtype=jnp.int32)
+    scale = 1.0 / math.sqrt(HEAD_DIM)
+    down_flattened = adapter_down.reshape(3 * ADAPTER_RANK, adapter_down.shape[2])
+
+    def to_ends(first_part, last_part):
+        sent = jnp.where(width_index == 0, last_part, first_part)
+        received = None
+        for hop in range(last):
+            if hop:
+                own = jnp.where(width_index == hop, last_part, first_part)
+                sent = (own.astype(jnp.float32) + received.astype(jnp.float32)).astype(jnp.bfloat16)
+            received = lax.ppermute(sent, "width", hops[hop])
+        return jnp.where(is_last, last_part, first_part), received
+
+    def from_ends(own):
+        first_side = own
+        last_side = own
+        received = own
+        for hop in range(last):
+            received = lax.ppermute(received, "width", hops[hop])
+            first_side = jnp.where(width_index == hop + 1, received, first_side)
+            last_side = jnp.where(width_index == last - 1 - hop, received, last_side)
+        return first_side, last_side
+
+    def mine(columns_of):
+        half = columns_of.shape[-1] // 2
+        return jnp.where(is_last, columns_of[..., half:], columns_of[..., :half])
+
+    def product(left, right):
+        return jnp.dot(left, right, preferred_element_type=jnp.float32).astype(jnp.bfloat16)
+
+    key_value_parts = [product(hidden_full, key_value_frozen_weight[i]) for i in range(2)]
+    own_kv, add_kv = to_ends(
+        *[
+            jnp.concatenate([part[:, side * HEAD_DIM : (side + 1) * HEAD_DIM] for part in key_value_parts], 1)
+            for side in range(2)
+        ]
+    )
+    rank_sum, upstream_sum = lax.psum(
+        (contract_last(hidden_full, down_flattened), contract_last(upstream_full, output_up)), "width"
+    )
+    low = rank_sum.astype(jnp.bfloat16)
+    out_rank = upstream_sum.astype(jnp.bfloat16)
+    low_q = low[:, :ADAPTER_RANK]
+    low_k = low[:, ADAPTER_RANK : 2 * ADAPTER_RANK]
+    low_v = low[:, 2 * ADAPTER_RANK :]
+    streams = []
+    for chunk in range(chunks):
+        spans = [
+            slice(side * group_cols + chunk * chunk_cols, side * group_cols + (chunk + 1) * chunk_cols)
+            for side in range(2)
+        ]
+        query_stream = to_ends(*[product(hidden_full, query_frozen_weight[:, s]) for s in spans])
+        grad_stream = to_ends(
+            *[contract_last(upstream_full, output_frozen_weight[s]).astype(jnp.bfloat16) for s in spans]
+        )
+        streams.append((query_stream, grad_stream))
+    kv_sum = own_kv.astype(jnp.float32) + add_kv.astype(jnp.float32)
+    key_up, value_up = mine(key_value_up_maps)
+    key_state = rotate(
+        kv_sum[:, :HEAD_DIM]
+        + adapter_scale * jnp.dot(low_k, key_up, preferred_element_type=jnp.float32),
+        positions, 0, 1.0,
+    ).astype(jnp.bfloat16)
+    value_state = (
+        kv_sum[:, HEAD_DIM:]
+        + adapter_scale * jnp.dot(low_v, value_up, preferred_element_type=jnp.float32)
+    ).astype(jnp.bfloat16)
+    head_dims = jnp.arange(HEAD_DIM, dtype=jnp.int32)
+    frequency = jnp.exp(
+        (head_dims - head_dims % 2).astype(jnp.float32) * (-math.log(rope_base) / HEAD_DIM)
+    )
+    angles = positions.astype(jnp.float32)[:, None] * frequency[None, :]
+    cosine, sine = jnp.cos(angles), jnp.sin(angles)
+    my_up = mine(query_up_map)
+    my_down = mine(output_down_map)
+    attentions, query_sides = [], []
+    key_total = value_total = 0.0
+    for chunk, ((own_q, add_q), (own_g, add_g)) in enumerate(streams):
+        cols = slice(chunk * chunk_cols, (chunk + 1) * chunk_cols)
+        attention, query_grad, key_term, value_term = attend(
+            scale, own_q, add_q, low_q, my_up[:, cols], own_g, add_g, out_rank, my_down[:, cols],
+            key_state, value_state, cosine, sine,
+        )
+        attentions.append(attention)
+        key_total += key_term
+        value_total += value_term
+        query_sides.append(from_ends(query_grad))
+    attention = jnp.concatenate(attentions, 1)
+    key_value_grad = jnp.concatenate(
+        [
+            rotate(key_total, positions, 0, -1.0).astype(jnp.bfloat16),
+            value_total.astype(jnp.bfloat16),
+        ],
+        1,
+    )
+    kv_sides = from_ends(key_value_grad)
+    key_grad = jnp.concatenate([side[:, :HEAD_DIM] for side in kv_sides], 1)
+    value_grad = jnp.concatenate([side[:, HEAD_DIM:] for side in kv_sides], 1)
+    query_grad = jnp.concatenate([sides[i] for i in range(2) for sides in query_sides], 1)
+
+    outer_terms = jnp.where(is_end, contract_last(attention, my_down), 0.0)
+    outer_rank = lax.psum(outer_terms, ("ffn", "width")).astype(jnp.bfloat16)
+    down_grad_part = contract_leading(out_rank, attention)
+    output_down_map_gradient = adapter_scale * lax.psum(
+        jnp.concatenate(
+            [
+                jnp.where(width_index == 0, down_grad_part, 0.0),
+                jnp.where(is_last, down_grad_part, 0.0),
+            ],
+            1,
+        ),
+        "width",
+    )
+    output_up_map_gradient = adapter_scale * contract_leading(outer_rank, upstream_full)
+
+    rank_terms = jnp.concatenate(
+        [
+            contract_last(query_grad, query_up_map),
+            contract_last(key_grad, key_value_up_maps[0]),
+            contract_last(value_grad, key_value_up_maps[1]),
+        ],
+        axis=1,
+    )
+    rank_gradient = lax.psum(rank_terms, "ffn").astype(jnp.bfloat16)
+    input_sums = []
+    out_cols = query_frozen_weight.shape[0] // PIECES
+    for piece in range(PIECES):
+        rows = slice(piece * out_cols, (piece + 1) * out_cols)
+        total = (
+            contract_last(query_grad, query_frozen_weight[rows])
+            + contract_last(key_grad, key_value_frozen_weight[0, rows])
+            + contract_last(value_grad, key_value_frozen_weight[1, rows])
+        ).astype(jnp.bfloat16)
+        input_sums.append(scatter_tokens(total, "ffn"))
+    own_rows = token_count // ffn_count
+    rank_rows = lax.dynamic_slice_in_dim(rank_gradient, ffn_index * own_rows, own_rows, 0)
+    hidden_gradient = (
+        jnp.concatenate(input_sums, 1)
+        + adapter_scale * jnp.dot(rank_rows, down_flattened, preferred_element_type=jnp.float32)
+    ).astype(jnp.bfloat16)
+    down_map_gradient = (adapter_scale * contract_leading(rank_gradient, hidden_full)).reshape(
+        adapter_down.shape
+    )
+    query_up_map_gradient = adapter_scale * contract_leading(low_q, query_grad)
+    key_value_up_maps_gradient = adapter_scale * jnp.stack(
+        [contract_leading(low_k, key_grad), contract_leading(low_v, value_grad)]
+    )
+    return (
+        hidden_gradient,
+        down_map_gradient,
+        query_up_map_gradient,
+        key_value_up_maps_gradient,
+        output_down_map_gradient,
+        output_up_map_gradient,
+    )
+
+
+def by_shape(*arrays):
+    ffn_count = lax.axis_size("ffn")
+    width_count = lax.axis_size("width")
+    group_cols = arrays[2].shape[1] // 2
+    fits = (
+        arrays[3].shape[2] == 2 * HEAD_DIM
+        and width_count % 2 == 0
+        and ffn_count & (ffn_count - 1) == 0
+        and group_cols % (HEAD_DIM * CHUNK_HEADS) == 0
+        and (arrays[0].shape[0] * ffn_count) % (BLOCKS * HEAD_DIM) == 0
+        and arrays[2].shape[0] % (PIECES * HEAD_DIM) == 0
+    )
+    return end_streams(*arrays) if fits else shards(*arrays)
+
+
 def solution(mesh):
     placed = (
         P(("groups", "ffn"), "width"),
@@ -267,7 +592,7 @@
         P("groups", "width"),
     )
     return jax.shard_map(
-        shards,
+        by_shape,
         mesh=mesh,
         in_specs=placed,
         out_specs=(

time: 599 us -> 659 us (1.10)
  starting transfers between devices: 0.37 us -> 67.7 us
  matrix products: 118 us -> 64.7 us
  Pallas kernels: 0 us -> 34.7 us
  local copies, waits for them, and re-layouts: 44.9 us -> 17.1 us
  blocking collectives: 159 us -> 176 us
  waiting for transfers between devices: 219 us -> 230 us
    ppermute x0 -> x50, waiting for transfers between devices: none -> 230 us  [the longest x27 118 us: to_ends(): received = lax.ppermute(sent, 'width', hops[hop])]
    reduce_scatter x5 -> x0, waiting for transfers between devices: 111 us -> none  [the longest x1 66.6 us: shards(): lax.psum_scatter(out_part.astype(jnp.bfloat16), 'width', scatter_dimensio...]
    all_gather x3 -> x0, waiting for transfers between devices: 106 us -> none  [the longest x1 55.6 us: shards(): lax.all_gather(query_block_grad, 'width', axis=0, tiled=True)]
    psum x3, blocking collectives: 106 us -> 176 us  [the longest x1 98.8 us: end_streams(): outer_rank = lax.psum(outer_terms, ('ffn', 'width')).astype(jnp.bfloat16)]
    ppermute x0 -> x50, starting transfers between devices: none -> 67.6 us  [the longest x27 37.6 us: to_ends(): received = lax.ppermute(sent, 'width', hops[hop])]
    all_gather x3 -> x0, blocking collectives: 53.1 us -> none  [the longest x1 19.7 us: shards(): lax.all_gather(value_block, 'width', axis=0, tiled=True)]
    pallas_call x0 -> x4, Pallas kernels: none -> 34.7 us  [attend(): pl.pallas_call(functools.partial(causal_heads, scale), out_shape=(jax.Sha...]
    dot_general x13, matrix products: 53.3 us -> 19.4 us  [the longest x10 17.4 us: product(): jnp.dot(left, right, preferred_element_type=jnp.float32)]
  transfers between devices with their start and end apart: 9 -> 51, of which waited for: 5 -> 16; matrix products, arithmetic and copies ran while one was open for 19% -> 11% of each run, Pallas kernels for 0% -> 4%
where the time goes in v1:
time: 659 us; the launch traced here: 646 us
  waiting for transfers between devices  230 us (35%)
  blocking collectives  176 us (27%)
  starting transfers between devices  67.7 us (10%)
  matrix products  64.7 us (10%)
  other arithmetic  39.5 us (6%)
  Pallas kernels  34.7 us (5%)
  local copies, waits for them, and re-layouts  17.1 us (3%)
  between operations  16.2 us (2%)
    ppermute x27, waiting for transfers between devices, to_ends(): received = lax.ppermute(sent, 'width', hops[hop])  118 us
    psum x1, blocking collectives, end_streams(): outer_rank = lax.psum(outer_terms, ('ffn', 'width')).astype(jnp.bfloat16)  98.8 us
    psum x1, blocking collectives, end_streams(): lax.psum((contract_last(hidden_full, down_flattened), contract_last(upstr...  63.9 us
    ppermute x8, waiting for transfers between devices, from_partner(): lax.ppermute(array, axis, [(i, i ^ 1 << bit) for i in range(lax.axis_size...  61.4 us
    ppermute x15, waiting for transfers between devices, from_ends(): received = lax.ppermute(received, 'width', hops[hop])  49.9 us
    ppermute x27, starting transfers between devices, to_ends(): received = lax.ppermute(sent, 'width', hops[hop])  37.6 us
    dot_general x20, matrix products, contract_last(): lax.dot_general(left_side, right_side, (((1,), (1,)), ((), ())), preferre...  35.5 us
    pallas_call x4, Pallas kernels, attend(): pl.pallas_call(functools.partial(causal_heads, scale), out_shape=(jax.Sha...  34.7 us
  transfers between devices with their start and end apart: 51, of which 16 were waited for; matrix products, arithmetic and copies ran while one was open for 11% of the time, Pallas kernels for 4%

profile of v1, /device:TPU:0, one launch (start us, length us, event | category | flops | bytes accessed | tf_op | source)
XLA Modules:
  0.0 645.8 jit_solution(3093063519604104008)
XLA Ops:
  10.3 24.2 %collective-permute-done = bf16[256,2048]{1,0:T(8,128)(2,1)} collective-permute-done((bf16[256,2048]{1,0:T(8,128)(2,1)}, bf16[256,2048]{1,0:T(8,128)(2,1)}, u32[]{:S(2)}, u32[]{:S(2)}) %collective-permute-start) | collective-permute-done | bytes 1048608 | tf_op jit(solution)/shard_map/ppermute | solution.py:24
  37.9 18.3 %collective-permute-done.5 = bf16[256,2048]{1,0:T(8,128)(2,1)} collective-permute-done((bf16[256,2048]{1,0:T(8,128)(2,1)}, bf16[256,2048]{1,0:T(8,128)(2,1)}, u32[]{:S(2)}, u32[]{:S(2)}) %collective-permute-start.5) | collective-permute-done | bytes 1048608 | tf_op jit(solution)/shard_map/ppermute | solution.py:24
  88.6 4.5 collective-permute-start.19
  123.8 63.9 %all-reduce.6 = (bf16[1024,48]{1,0:T(8,128)(2,1)S(1)}, bf16[1024,16]{1,0:T(8,128)(2,1)S(1)}) all-reduce(f32[1024,48]{1,0:T(8,128)} %fusion.83, f32[1024,16]{1,0:T(8,128)} %fusion.84), channel_id=1, replica_groups=mesh['groups'=2,'ffn'=4,'width'=4] {'width'}, use_global_device_ids=true, to_apply=%region_0.1 | all-reduce | flops 65536 | bytes 393216 | tf_op jit(solution)/shard_map/psum | solution.py:446
  205.3 8.2 %collective-permute-done.25 = bf16[1024,256]{1,0:T(8,128)(2,1)S(1)} collective-permute-done((bf16[1024,256]{1,0:T(8,128)(2,1)}, bf16[1024,256]{1,0:T(8,128)(2,1)S(1)}, u32[]{:S(2)}, u32[]{:S(2)}) %collective-permute-start.25) | collective-permute-done | bytes 524320 | tf_op jit(solution)/shard_map/ppermute | solution.py:419
  214.4 10.2 %collective-permute-done.37 = bf16[1024,256]{1,0:T(8,128)(2,1)S(1)} collective-permute-done((bf16[1024,256]{1,0:T(8,128)(2,1)S(1)}, bf16[1024,256]{1,0:T(8,128)(2,1)S(1)}, u32[]{:S(2)}, u32[]{:S(2)}) %collective-permute-start.37) | collective-permute-done | bytes 524320 | tf_op jit(solution)/shard_map/ppermute | solution.py:419
  225.5 8.6 %collective-permute-done.34 = bf16[1024,256]{1,0:T(8,128)(2,1)S(1)} collective-permute-done((bf16[1024,256]{1,0:T(8,128)(2,1)S(1)}, bf16[1024,256]{1,0:T(8,128)(2,1)S(1)}, u32[]{:S(2)}, u32[]{:S(2)}) %collective-permute-start.34) | collective-permute-done | bytes 524320 | tf_op jit(solution)/shard_map/ppermute | solution.py:419
  246.5 67.7 %collective-permute-done.12 = bf16[1024,256]{1,0:T(8,128)(2,1)S(1)} collective-permute-done((bf16[1024,256]{1,0:T(8,128)(2,1)S(1)}, bf16[1024,256]{1,0:T(8,128)(2,1)S(1)}, u32[]{:S(2)}, u32[]{:S(2)}) %collective-permute-start.12) | collective-permute-done | bytes 524320 | tf_op jit(solution)/shard_map/ppermute | solution.py:419
  316.4 4.3 multiply_sine_fusion
  323.6 8.6 %shard_map.146 = (bf16[1024,256]{1,0:T(8,128)(2,1)S(1)}, bf16[1024,256]{1,0:T(8,128)(2,1)S(1)}, f32[1024,128]{1,0:T(8,128)S(1)}, f32[1024,128]{1,0:T(8,128)S(1)}) custom-call(bf16[1024,256]{1,0:T(8,128)(2,1)S(1)} %copy-done.4, bf16[1024,256]{1,0:T(8,128)(2,1)S(1)} %collective-permute-done.18.add_q, bf16[1024,16]{1,0:T(8,128)(2,1)S(1)} %bitcast.127, ...), custom_call_target="tpu_custom_call" | custom-call | flops 3221225472 | bytes 4194304 | tf_op jit(solution)/shard_map/pallas_call | solution.py:333
  336.7 8.6 %shard_map.145 = (bf16[1024,256]{1,0:T(8,128)(2,1)S(1)}, bf16[1024,256]{1,0:T(8,128)(2,1)S(1)}, f32[1024,128]{1,0:T(8,128)S(1)}, f32[1024,128]{1,0:T(8,128)S(1)}) custom-call(bf16[1024,256]{1,0:T(8,128)(2,1)S(1)} %copy-done.5, bf16[1024,256]{1,0:T(8,128)(2,1)S(1)} %collective-permute-done.4.add_q, bf16[1024,16]{1,0:T(8,128)(2,1)S(1)} %bitcast.128, ...), custom_call_target="tpu_custom_call" | custom-call | flops 3221225472 | bytes 4194304 | tf_op jit(solution)/shard_map/pallas_call | solution.py:333
  347.9 11.2 %collective-permute-done.27.add_q = bf16[1024,256]{1,0:T(8,128)(2,1)S(1)} collective-permute-done((bf16[1024,256]{1,0:T(8,128)(2,1)S(1)}, bf16[1024,256]{1,0:T(8,128)(2,1)S(1)}, u32[]{:S(2)}, u32[]{:S(2)}) %collective-permute-start.27) | collective-permute-done | bytes 524320 | tf_op jit(solution)/shard_map/ppermute | solution.py:419
  359.1 8.8 %shard_map.147 = (bf16[1024,256]{1,0:T(8,128)(2,1)S(1)}, bf16[1024,256]{1,0:T(8,128)(2,1)S(1)}, f32[1024,128]{1,0:T(8,128)S(1)}, f32[1024,128]{1,0:T(8,128)S(1)}) custom-call(bf16[1024,256]{1,0:T(8,128)(2,1)S(1)} %copy-done.3, bf16[1024,256]{1,0:T(8,128)(2,1)S(1)} %collective-permute-done.27.add_q, bf16[1024,16]{1,0:T(8,128)(2,1)S(1)} %bitcast.129, ...), custom_call_target="tpu_custom_call" | custom-call | flops 3221225472 | bytes 4194304 | tf_op jit(solution)/shard_map/pallas_call | solution.py:333
  367.9 4.2 collective-permute-done.36.add_q
  372.1 8.6 %shard_map.148 = (bf16[1024,256]{1,0:T(8,128)(2,1)S(1)}, bf16[1024,256]{1,0:T(8,128)(2,1)S(1)}, f32[1024,128]{1,0:T(8,128)S(1)}, f32[1024,128]{1,0:T(8,128)S(1)}) custom-call(bf16[1024,256]{1,0:T(8,128)(2,1)S(1)} %copy-done.1, bf16[1024,256]{1,0:T(8,128)(2,1)S(1)} %collective-permute-done.36.add_q, bf16[1024,16]{1,0:T(8,128)(2,1)S(1)} %bitcast.130, ...), custom_call_target="tpu_custom_call" | custom-call | flops 3221225472 | bytes 4194304 | tf_op jit(solution)/shard_map/pallas_call | solution.py:333
  402.9 98.8 %psum.39 = bf16[1024,16]{1,0:T(8,128)(2,1)S(1)} all-reduce(f32[1024,16]{1,0:T(8,128)} %convolution_select_fusion), channel_id=1, replica_groups=mesh['groups'=2,'ffn'=4,'width'=4] {'ffn','width'}, use_global_device_ids=true, to_apply=%region_4.5 | all-reduce | flops 16384 | bytes 98304 | tf_op jit(solution)/shard_map/psum | solution.py:510
  519.4 6.2 collective-permute-done.45
  527.5 42.0 %collective-permute-done.15 = bf16[1024,256]{1,0:T(8,128)(2,1)S(1)} collective-permute-done((bf16[1024,256]{1,0:T(8,128)(2,1)}, bf16[1024,256]{1,0:T(8,128)(2,1)S(1)}, u32[]{:S(2)}, u32[]{:S(2)}) %collective-permute-start.15) | collective-permute-done | bytes 524320 | tf_op jit(solution)/shard_map/ppermute | solution.py:427
  577.7 4.5 fusion.2
  583.0 4.8 fusion
  593.6 13.5 %all-reduce.7 = bf16[1024,48]{0,1:T(8,128)(2,1)S(1)} all-reduce(f32[1024,48]{0,1:T(8,128)S(1)} %pad_maximum_fusion.8), channel_id=1, replica_groups=mesh['groups'=2,'ffn'=4,'width'=4] {'ffn'}, use_global_device_ids=true, to_apply=%region_2.3 | all-reduce | flops 49152 | bytes 294912 | tf_op jit(solution)/shard_map/psum | solution.py:532
  607.1 3.9 convolution_multiply_fusion.1
  617.9 9.6 %collective-permute-done.47 = bf16[256,1024]{1,0:T(8,128)(2,1)S(1)} collective-permute-done((bf16[256,1024]{1,0:T(8,128)(2,1)S(1)}, bf16[256,1024]{1,0:T(8,128)(2,1)S(1)}, u32[]{:S(2)}, u32[]{:S(2)}) %collective-permute-start.47) | collective-permute-done | bytes 524320 | tf_op jit(solution)/shard_map/ppermute | solution.py:24
  627.7 9.2 %collective-permute-done.49 = bf16[256,1024]{1,0:T(8,128)(2,1)S(1)} collective-permute-done((bf16[256,1024]{1,0:T(8,128)(2,1)S(1)}, bf16[256,1024]{1,0:T(8,128)(2,1)S(1)}, u32[]{:S(2)}, u32[]{:S(2)}) %collective-permute-start.49) | collective-permute-done | bytes 524320 | tf_op jit(solution)/shard_map/ppermute | solution.py:24
  (317 shorter events, 176.8 us)
Async XLA Ops:
  7.2 505.3 %all-reduce.5.cloned.1.call-start = ((), (), s32[]{:S(2)}) async-start(), calls=%async_computation | async-start | bytes 262144 | tf_op jit(solution)/shard_map/psum | solution.py:512
  10.3 45.9 %collective-permute-start.5 = (bf16[256,2048]{1,0:T(8,128)(2,1)}, bf16[256,2048]{1,0:T(8,128)(2,1)}, u32[]{:S(2)}, u32[]{:S(2)}) collective-permute-start(bf16[256,2048]{1,0:T(8,128)(2,1)} %param.11), channel_id=1, source_target_pairs={{0,8},{4,12},{8,0},{12,4},{1,9},{5,13},{9,1},{13,5},{2,10},{6,14},... | collective-permute-start | bytes 3145736 | tf_op jit(solution)/shard_map/ppermute | solution.py:24
  88.6 99.2 %collective-permute-start.19 = (bf16[1024,256]{1,0:T(8,128)(2,1)}, bf16[1024,256]{1,0:T(8,128)(2,1)}, u32[]{:S(2)}, u32[]{:S(2)}) collective-permute-start(bf16[1024,256]{1,0:T(8,128)(2,1)} %get-tuple-element.58), channel_id=1, source_target_pairs={{0,1},{3,2},{4,5},{7,6},{8,9},{11,10},{12,13},{15,14},{16,17},{19,... | collective-permute-start | bytes 1572872 | tf_op jit(solution)/shard_map/ppermute | solution.py:419
  95.6 95.6 %collective-permute-start.16 = (bf16[1024,256]{1,0:T(8,128)(2,1)}, bf16[1024,256]{1,0:T(8,128)(2,1)}, u32[]{:S(2)}, u32[]{:S(2)}) collective-permute-start(bf16[1024,256]{1,0:T(8,128)(2,1)} %get-tuple-element.60), channel_id=1, source_target_pairs={{0,1},{3,2},{4,5},{7,6},{8,9},{11,10},{12,13},{15,14},{16,17},{19,... | collective-permute-start | bytes 1572872 | tf_op jit(solution)/shard_map/ppermute | solution.py:419
  98.9 104.3 %collective-permute-start.10 = (bf16[1024,256]{1,0:T(8,128)(2,1)}, bf16[1024,256]{1,0:T(8,128)(2,1)}, u32[]{:S(2)}, u32[]{:S(2)}) collective-permute-start(bf16[1024,256]{1,0:T(8,128)(2,1)} %broadcast_select_fusion.6), channel_id=1, source_target_pairs={{0,1},{3,2},{4,5},{7,6},{8,9},{11,10},{12,13},{15,14},{16,17},{19,... | collective-permute-start | bytes 1572872 | tf_op jit(solution)/shard_map/ppermute | solution.py:419
  105.3 88.6 %collective-permute-start.7 = (bf16[1024,256]{1,0:T(8,128)(2,1)}, bf16[1024,256]{1,0:T(8,128)(2,1)}, u32[]{:S(2)}, u32[]{:S(2)}) collective-permute-start(bf16[1024,256]{1,0:T(8,128)(2,1)} %get-tuple-element.62), channel_id=1, source_target_pairs={{0,1},{3,2},{4,5},{7,6},{8,9},{11,10},{12,13},{15,14},{16,17},{19,... | collective-permute-start | bytes 1572872 | tf_op jit(solution)/shard_map/ppermute | solution.py:419
  109.8 86.8 %collective-permute-start.2 = (bf16[1024,256]{1,0:T(8,128)(2,1)}, bf16[1024,256]{1,0:T(8,128)(2,1)}, u32[]{:S(2)}, u32[]{:S(2)}) collective-permute-start(bf16[1024,256]{1,0:T(8,128)(2,1)} %get-tuple-element.64), channel_id=1, source_target_pairs={{0,1},{3,2},{4,5},{7,6},{8,9},{11,10},{12,13},{15,14},{16,17},{19,... | collective-permute-start | bytes 1572872 | tf_op jit(solution)/shard_map/ppermute | solution.py:419
  238.7 82.2 %collective-permute-start.21 = (bf16[1024,256]{1,0:T(8,128)(2,1)S(1)}, bf16[1024,256]{1,0:T(8,128)(2,1)S(1)}, u32[]{:S(2)}, u32[]{:S(2)}) collective-permute-start(bf16[1024,256]{1,0:T(8,128)(2,1)S(1)} %add_convert_fusion.10), channel_id=1, source_target_pairs={{2,3},{1,0},{6,7},{5,4},{10,11},{9,8},{14,15},{13,12},{18,19},{17,... | collective-permute-start | bytes 1572872 | tf_op jit(solution)/shard_map/ppermute | solution.py:419
  240.3 82.0 %collective-permute-start.18 = (bf16[1024,256]{1,0:T(8,128)(2,1)S(1)}, bf16[1024,256]{1,0:T(8,128)(2,1)S(1)}, u32[]{:S(2)}, u32[]{:S(2)}) collective-permute-start(bf16[1024,256]{1,0:T(8,128)(2,1)S(1)} %add_convert_fusion.12), channel_id=1, source_target_pairs={{2,3},{1,0},{6,7},{5,4},{10,11},{9,8},{14,15},{13,12},{18,19},{17,... | collective-permute-start | bytes 1572872 | tf_op jit(solution)/shard_map/ppermute | solution.py:419
  241.8 72.4 %collective-permute-start.12 = (bf16[1024,256]{1,0:T(8,128)(2,1)S(1)}, bf16[1024,256]{1,0:T(8,128)(2,1)S(1)}, u32[]{:S(2)}, u32[]{:S(2)}) collective-permute-start(bf16[1024,256]{1,0:T(8,128)(2,1)S(1)} %add_convert_fusion.14), channel_id=1, source_target_pairs={{2,3},{1,0},{6,7},{5,4},{10,11},{9,8},{14,15},{13,12},{18,19},{17,... | collective-permute-start | bytes 1572872 | tf_op jit(solution)/shard_map/ppermute | solution.py:419
  243.3 88.9 %collective-permute-start.9 = (bf16[1024,256]{1,0:T(8,128)(2,1)S(1)}, bf16[1024,256]{1,0:T(8,128)(2,1)S(1)}, u32[]{:S(2)}, u32[]{:S(2)}) collective-permute-start(bf16[1024,256]{1,0:T(8,128)(2,1)S(1)} %add_convert_fusion.16), channel_id=1, source_target_pairs={{2,3},{1,0},{6,7},{5,4},{10,11},{9,8},{14,15},{13,12},{18,19},{17,... | collective-permute-start | bytes 1572872 | tf_op jit(solution)/shard_map/ppermute | solution.py:419
  245.0 91.7 %collective-permute-start.4 = (bf16[1024,256]{1,0:T(8,128)(2,1)S(1)}, bf16[1024,256]{1,0:T(8,128)(2,1)S(1)}, u32[]{:S(2)}, u32[]{:S(2)}) collective-permute-start(bf16[1024,256]{1,0:T(8,128)(2,1)S(1)} %add_convert_fusion.18), channel_id=1, source_target_pairs={{2,3},{1,0},{6,7},{5,4},{10,11},{9,8},{14,15},{13,12},{18,19},{17,... | collective-permute-start | bytes 1572872 | tf_op jit(solution)/shard_map/ppermute | solution.py:419
  321.0 38.2 %collective-permute-start.27 = (bf16[1024,256]{1,0:T(8,128)(2,1)S(1)}, bf16[1024,256]{1,0:T(8,128)(2,1)S(1)}, u32[]{:S(2)}, u32[]{:S(2)}) collective-permute-start(bf16[1024,256]{1,0:T(8,128)(2,1)S(1)} %add_convert_fusion.8), channel_id=1, source_target_pairs={{2,3},{1,0},{6,7},{5,4},{10,11},{9,8},{14,15},{13,12},{18,19},{17,... | collective-permute-start | bytes 1572872 | tf_op jit(solution)/shard_map/ppermute | solution.py:419
  322.3 45.6 %collective-permute-start.39 = (bf16[1024,256]{1,0:T(8,128)(2,1)S(1)}, bf16[1024,256]{1,0:T(8,128)(2,1)S(1)}, u32[]{:S(2)}, u32[]{:S(2)}) collective-permute-start(bf16[1024,256]{1,0:T(8,128)(2,1)S(1)} %add_convert_fusion.2), channel_id=1, source_target_pairs={{2,3},{1,0},{6,7},{5,4},{10,11},{9,8},{14,15},{13,12},{18,19},{17,... | collective-permute-start | bytes 1572872 | tf_op jit(solution)/shard_map/ppermute | solution.py:419
  332.3 39.9 %collective-permute-start.36 = (bf16[1024,256]{1,0:T(8,128)(2,1)S(1)}, bf16[1024,256]{1,0:T(8,128)(2,1)S(1)}, u32[]{:S(2)}, u32[]{:S(2)}) collective-permute-start(bf16[1024,256]{1,0:T(8,128)(2,1)S(1)} %add_convert_fusion.4), channel_id=1, source_target_pairs={{2,3},{1,0},{6,7},{5,4},{10,11},{9,8},{14,15},{13,12},{18,19},{17,... | collective-permute-start | bytes 1572872 | tf_op jit(solution)/shard_map/ppermute | solution.py:419
  386.2 115.6 %collective-permute-start.40 = (bf16[1024,256]{1,0:T(8,128)(2,1)S(1)}, bf16[1024,256]{1,0:T(8,128)(2,1)}, u32[]{:S(2)}, u32[]{:S(2)}) collective-permute-start(bf16[1024,256]{1,0:T(8,128)(2,1)S(1)} %get-tuple-element.25), channel_id=1, source_target_pairs={{0,1},{3,2},{4,5},{7,6},{8,9},{11,10},{12,13},{15,14},{16,17},{19,... | collective-permute-start | bytes 1572872 | tf_op jit(solution)/shard_map/ppermute | solution.py:427
  388.3 115.0 %collective-permute-start.31 = (bf16[1024,256]{1,0:T(8,128)(2,1)S(1)}, bf16[1024,256]{1,0:T(8,128)(2,1)}, u32[]{:S(2)}, u32[]{:S(2)}) collective-permute-start(bf16[1024,256]{1,0:T(8,128)(2,1)S(1)} %get-tuple-element.24), channel_id=1, source_target_pairs={{0,1},{3,2},{4,5},{7,6},{8,9},{11,10},{12,13},{15,14},{16,17},{19,... | collective-permute-start | bytes 1572872 | tf_op jit(solution)/shard_map/ppermute | solution.py:427
  390.4 114.3 %collective-permute-start.22 = (bf16[1024,256]{1,0:T(8,128)(2,1)S(1)}, bf16[1024,256]{1,0:T(8,128)(2,1)}, u32[]{:S(2)}, u32[]{:S(2)}) collective-permute-start(bf16[1024,256]{1,0:T(8,128)(2,1)S(1)} %get-tuple-element.23), channel_id=1, source_target_pairs={{0,1},{3,2},{4,5},{7,6},{8,9},{11,10},{12,13},{15,14},{16,17},{19,... | collective-permute-start | bytes 1572872 | tf_op jit(solution)/shard_map/ppermute | solution.py:427
  392.5 113.7 %collective-permute-start.13 = (bf16[1024,256]{1,0:T(8,128)(2,1)S(1)}, bf16[1024,256]{1,0:T(8,128)(2,1)}, u32[]{:S(2)}, u32[]{:S(2)}) collective-permute-start(bf16[1024,256]{1,0:T(8,128)(2,1)S(1)} %get-tuple-element.22), channel_id=1, source_target_pairs={{0,1},{3,2},{4,5},{7,6},{8,9},{11,10},{12,13},{15,14},{16,17},{19,... | collective-permute-start | bytes 1572872 | tf_op jit(solution)/shard_map/ppermute | solution.py:427
  397.7 109.9 %collective-permute-start.44 = (bf16[1024,256]{1,0:T(8,128)(2,1)}, bf16[1024,256]{1,0:T(8,128)(2,1)}, u32[]{:S(2)}, u32[]{:S(2)}) collective-permute-start(bf16[1024,256]{1,0:T(8,128)(2,1)} %collective-permute-done.43), channel_id=1, source_target_pairs={{1,2},{2,1},{5,6},{6,5},{9,10},{10,9},{13,14},{14,13},{17,18},{18,... | collective-permute-start | bytes 1572872 | tf_op jit(solution)/shard_map/ppermute | solution.py:427
  514.0 58.1 %collective-permute-start.42 = (bf16[1024,256]{1,0:T(8,128)(2,1)}, bf16[1024,256]{1,0:T(8,128)(2,1)S(1)}, u32[]{:S(2)}, u32[]{:S(2)}) collective-permute-start(bf16[1024,256]{1,0:T(8,128)(2,1)} %collective-permute-done.41), channel_id=1, source_target_pairs={{2,3},{1,0},{6,7},{5,4},{10,11},{9,8},{14,15},{13,12},{18,19},{17,... | collective-permute-start | bytes 1572872 | tf_op jit(solution)/shard_map/ppermute | solution.py:427
  515.3 54.9 %collective-permute-start.33 = (bf16[1024,256]{1,0:T(8,128)(2,1)}, bf16[1024,256]{1,0:T(8,128)(2,1)S(1)}, u32[]{:S(2)}, u32[]{:S(2)}) collective-permute-start(bf16[1024,256]{1,0:T(8,128)(2,1)} %collective-permute-done.32), channel_id=1, source_target_pairs={{2,3},{1,0},{6,7},{5,4},{10,11},{9,8},{14,15},{13,12},{18,19},{17,... | collective-permute-start | bytes 1572872 | tf_op jit(solution)/shard_map/ppermute | solution.py:427
  516.6 53.2 %collective-permute-start.24 = (bf16[1024,256]{1,0:T(8,128)(2,1)}, bf16[1024,256]{1,0:T(8,128)(2,1)S(1)}, u32[]{:S(2)}, u32[]{:S(2)}) collective-permute-start(bf16[1024,256]{1,0:T(8,128)(2,1)} %collective-permute-done.23), channel_id=1, source_target_pairs={{2,3},{1,0},{6,7},{5,4},{10,11},{9,8},{14,15},{13,12},{18,19},{17,... | collective-permute-start | bytes 1572872 | tf_op jit(solution)/shard_map/ppermute | solution.py:427
  517.9 51.6 %collective-permute-start.15 = (bf16[1024,256]{1,0:T(8,128)(2,1)}, bf16[1024,256]{1,0:T(8,128)(2,1)S(1)}, u32[]{:S(2)}, u32[]{:S(2)}) collective-permute-start(bf16[1024,256]{1,0:T(8,128)(2,1)} %collective-permute-done.14), channel_id=1, source_target_pairs={{2,3},{1,0},{6,7},{5,4},{10,11},{9,8},{14,15},{13,12},{18,19},{17,... | collective-permute-start | bytes 1572872 | tf_op jit(solution)/shard_map/ppermute | solution.py:427
  (84 other events, 1459.1 us)
Sparse Core Ops, SparseCore 0:
  400.0 37.1 all-reduce.4

commit v2 on v1

--- a/solution.py
+++ b/solution.py
@@ -347,17 +347,10 @@
     )(*operands)
 
 
-def gather_tokens(block, axis):
-    count = lax.axis_size(axis)
-    index = lax.axis_index(axis)
-    held = block
-    for bit in reversed(range(count.bit_length() - 1)):
-        other = from_partner(held, axis, bit)
-        low_side = (index >> bit) % 2 == 0
-        held = jnp.stack([jnp.where(low_side, held, other), jnp.where(low_side, other, held)])
-    bits = count.bit_length() - 1
-    order = tuple(reversed(range(bits))) + (bits, bits + 1)
-    return held.transpose(order).reshape(count * block.shape[0], block.shape[1])
+def pair_sum(values, axis):
+    for bit in range(lax.axis_size(axis).bit_length() - 1):
+        values = values + from_partner(values, axis, bit)
+    return values
 
 
 def scatter_tokens(parts, axis):
@@ -398,8 +391,9 @@
     ]
     is_last = width_index == last
     is_end = (width_index == 0) | is_last
-    hidden_full = gather_tokens(hidden, "ffn")
-    upstream_full = gather_tokens(upstream, "ffn")
+    hidden_full = lax.all_gather(hidden, "ffn", axis=0, tiled=True)
+    upstream, hidden_full = lax.optimization_barrier((upstream, hidden_full))
+    upstream_full = lax.all_gather(upstream, "ffn", axis=0, tiled=True)
     token_count = hidden_full.shape[0]
     query_cols = query_frozen_weight.shape[1]
     group_cols = query_cols // 2
@@ -419,12 +413,25 @@
             received = lax.ppermute(sent, "width", hops[hop])
         return jnp.where(is_last, last_part, first_part), received
 
+    first_hops = []
+
+    def line_sum(own):
+        total = own.astype(jnp.float32)
+        received = None
+        for hop in range(last):
+            sent = own if hop == 0 else own + received
+            received = lax.ppermute(sent, "width", hops[hop])
+            total = total + received.astype(jnp.float32)
+        return total
+
     def from_ends(own):
         first_side = own
         last_side = own
         received = own
         for hop in range(last):
             received = lax.ppermute(received, "width", hops[hop])
+            if hop == 0:
+                first_hops.append(received)
             first_side = jnp.where(width_index == hop + 1, received, first_side)
             last_side = jnp.where(width_index == last - 1 - hop, received, last_side)
         return first_side, last_side
@@ -443,11 +450,10 @@
             for side in range(2)
         ]
     )
-    rank_sum, upstream_sum = lax.psum(
-        (contract_last(hidden_full, down_flattened), contract_last(upstream_full, output_up)), "width"
-    )
-    low = rank_sum.astype(jnp.bfloat16)
-    out_rank = upstream_sum.astype(jnp.bfloat16)
+    low = line_sum(contract_last(down_flattened, hidden_full).astype(jnp.bfloat16))
+    low = low.astype(jnp.bfloat16).T
+    out_rank = line_sum(contract_last(output_up, upstream_full).astype(jnp.bfloat16))
+    out_rank = out_rank.astype(jnp.bfloat16).T
     low_q = low[:, :ADAPTER_RANK]
     low_k = low[:, ADAPTER_RANK : 2 * ADAPTER_RANK]
     low_v = low[:, 2 * ADAPTER_RANK :]
@@ -485,6 +491,8 @@
     key_total = value_total = 0.0
     for chunk, ((own_q, add_q), (own_g, add_g)) in enumerate(streams):
         cols = slice(chunk * chunk_cols, (chunk + 1) * chunk_cols)
+        if chunk > 1:
+            add_q, first_hops[chunk - 2] = lax.optimization_barrier((add_q, first_hops[chunk - 2]))
         attention, query_grad, key_term, value_term = attend(
             scale, own_q, add_q, low_q, my_up[:, cols], own_g, add_g, out_rank, my_down[:, cols],
             key_state, value_state, cosine, sine,
@@ -506,30 +514,22 @@
     value_grad = jnp.concatenate([side[:, HEAD_DIM:] for side in kv_sides], 1)
     query_grad = jnp.concatenate([sides[i] for i in range(2) for sides in query_sides], 1)
 
-    outer_terms = jnp.where(is_end, contract_last(attention, my_down), 0.0)
-    outer_rank = lax.psum(outer_terms, ("ffn", "width")).astype(jnp.bfloat16)
-    down_grad_part = contract_leading(out_rank, attention)
-    output_down_map_gradient = adapter_scale * lax.psum(
-        jnp.concatenate(
-            [
-                jnp.where(width_index == 0, down_grad_part, 0.0),
-                jnp.where(is_last, down_grad_part, 0.0),
-            ],
-            1,
-        ),
-        "width",
+    outer_terms = jnp.where(is_end, contract_last(my_down, attention), 0.0)
+    outer_rank = pair_sum(line_sum(outer_terms), "ffn").astype(jnp.bfloat16).T
+    output_down_map_gradient = adapter_scale * jnp.concatenate(
+        from_ends(contract_leading(out_rank, attention)), 1
     )
     output_up_map_gradient = adapter_scale * contract_leading(outer_rank, upstream_full)
 
     rank_terms = jnp.concatenate(
         [
-            contract_last(query_grad, query_up_map),
-            contract_last(key_grad, key_value_up_maps[0]),
-            contract_last(value_grad, key_value_up_maps[1]),
+            contract_last(query_up_map, query_grad),
+            contract_last(key_value_up_maps[0], key_grad),
+            contract_last(key_value_up_maps[1], value_grad),
         ],
-        axis=1,
-    )
-    rank_gradient = lax.psum(rank_terms, "ffn").astype(jnp.bfloat16)
+        axis=0,
+    )
+    rank_gradient = pair_sum(rank_terms, "ffn").astype(jnp.bfloat16).T
     input_sums = []
     out_cols = query_frozen_weight.shape[0] // PIECES
     for piece in range(PIECES):

time: 659 us -> 518 us (0.79)
  the two profiles are of different devices: /device:TPU:0 before, /device:TPU:8 now
where the time goes in v2:
time: 518 us; the launch traced here: 508 us
  waiting for transfers between devices  214 us (41%)
  starting transfers between devices  115 us (22%)
  matrix products  81.1 us (16%)
  other arithmetic  37 us (7%)
  Pallas kernels  37 us (7%)
  between operations  15.9 us (3%)
  local copies, waits for them, and re-layouts  8.31 us (2%)
    ppermute x27, waiting for transfers between devices, to_ends(): received = lax.ppermute(sent, 'width', hops[hop])  76.9 us
    ppermute x27, starting transfers between devices, to_ends(): received = lax.ppermute(sent, 'width', hops[hop])  56.8 us
    ppermute x18, waiting for transfers between devices, from_ends(): received = lax.ppermute(received, 'width', hops[hop])  52.3 us
    dot_general x20, matrix products, contract_last(): lax.dot_general(left_side, right_side, (((1,), (1,)), ((), ())), preferre...  43.3 us
    pallas_call x4, Pallas kernels, attend(): pl.pallas_call(functools.partial(causal_heads, scale), out_shape=(jax.Sha...  37 us
    all_gather x1, waiting for transfers between devices, end_streams(): hidden_full = lax.all_gather(hidden, 'ffn', axis=0, tiled=True)  35.5 us
    ppermute x18, starting transfers between devices, from_ends(): received = lax.ppermute(received, 'width', hops[hop])  33.6 us
    ppermute x8, waiting for transfers between devices, from_partner(): lax.ppermute(array, axis, [(i, i ^ 1 << bit) for i in range(lax.axis_size...  30.7 us
  transfers between devices with their start and end apart: 64, of which 34 were waited for; matrix products, arithmetic and copies ran while one was open for 17% of the time, Pallas kernels for 6%

profile of v2, /device:TPU:8, one launch (start us, length us, event | category | flops | bytes accessed | tf_op | source)
XLA Modules:
  0.0 507.9 jit_solution(10950554634980917380)
XLA Ops:
  9.7 35.5 %all-gather.3.cloned.1.call-done = bf16[1024,2048]{1,0:T(8,128)(2,1)} async-done(((bf16[256,2048]{1,0:T(8,128)(2,1)}), bf16[1024,2048]{1,0:T(8,128)(2,1)}) %all-gather.3.cloned.1.call-update) | async-done | bytes 4194320 | tf_op jit(solution)/shard_map/all_gather | solution.py:394
  63.4 5.1 broadcast_select_fusion.5
  75.9 5.8 %collective-permute-done.3 = bf16[48,1024]{0,1:T(8,128)(2,1)S(1)} collective-permute-done((bf16[48,1024]{0,1:T(8,128)(2,1)S(1)}, bf16[48,1024]{0,1:T(8,128)(2,1)S(1)}, u32[]{:S(2)}, u32[]{:S(2)}) %collective-permute-start.3) | collective-permute-done | bytes 98336 | tf_op jit(solution)/shard_map/ppermute | solution.py:423
  119.1 6.9 %collective-permute-done.36 = bf16[1024,256]{1,0:T(8,128)(2,1)S(1)} collective-permute-done((bf16[1024,256]{1,0:T(8,128)(2,1)S(1)}, bf16[1024,256]{1,0:T(8,128)(2,1)S(1)}, u32[]{:S(2)}, u32[]{:S(2)}) %collective-permute-start.36) | collective-permute-done | bytes 524320 | tf_op jit(solution)/shard_map/ppermute | solution.py:413
  134.3 6.2 %collective-permute-done.1 = bf16[1024,256]{1,0:T(8,128)(2,1)S(1)} collective-permute-done((bf16[1024,256]{1,0:T(8,128)(2,1)S(1)}, bf16[1024,256]{1,0:T(8,128)(2,1)S(1)}, u32[]{:S(2)}, u32[]{:S(2)}) %collective-permute-start.1) | collective-permute-done | bytes 524320 | tf_op jit(solution)/shard_map/ppermute | solution.py:413
  142.8 8.9 %collective-permute-done.28 = bf16[1024,256]{1,0:T(8,128)(2,1)S(1)} collective-permute-done((bf16[1024,256]{1,0:T(8,128)(2,1)S(1)}, bf16[1024,256]{1,0:T(8,128)(2,1)S(1)}, u32[]{:S(2)}, u32[]{:S(2)}) %collective-permute-start.28) | collective-permute-done | bytes 524320 | tf_op jit(solution)/shard_map/ppermute | solution.py:413
  212.6 11.7 %collective-permute-done.6 = bf16[1024,256]{1,0:T(8,128)(2,1)S(1)} collective-permute-done((bf16[1024,256]{1,0:T(8,128)(2,1)S(1)}, bf16[1024,256]{1,0:T(8,128)(2,1)S(1)}, u32[]{:S(2)}, u32[]{:S(2)}) %collective-permute-start.6) | collective-permute-done | bytes 524320 | tf_op jit(solution)/shard_map/ppermute | solution.py:413
  225.8 8.5 %collective-permute-done.30 = bf16[1024,256]{1,0:T(8,128)(2,1)S(1)} collective-permute-done((bf16[1024,256]{1,0:T(8,128)(2,1)S(1)}, bf16[1024,256]{1,0:T(8,128)(2,1)S(1)}, u32[]{:S(2)}, u32[]{:S(2)}) %collective-permute-start.30) | collective-permute-done | bytes 524320 | tf_op jit(solution)/shard_map/ppermute | solution.py:413
  242.6 8.3 %collective-permute-done.7 = bf16[1024,256]{1,0:T(8,128)(2,1)S(1)} collective-permute-done((bf16[1024,256]{1,0:T(8,128)(2,1)S(1)}, bf16[1024,256]{1,0:T(8,128)(2,1)S(1)}, u32[]{:S(2)}, u32[]{:S(2)}) %collective-permute-start.7) | collective-permute-done | bytes 524320 | tf_op jit(solution)/shard_map/ppermute | solution.py:413
  253.6 6.4 %collective-permute-done.22 = bf16[1024,256]{1,0:T(8,128)(2,1)S(1)} collective-permute-done((bf16[1024,256]{1,0:T(8,128)(2,1)S(1)}, bf16[1024,256]{1,0:T(8,128)(2,1)S(1)}, u32[]{:S(2)}, u32[]{:S(2)}) %collective-permute-start.22) | collective-permute-done | bytes 524320 | tf_op jit(solution)/shard_map/ppermute | solution.py:413
  277.6 8.6 %shard_map.145 = (bf16[1024,256]{1,0:T(8,128)(2,1)S(1)}, bf16[1024,256]{1,0:T(8,128)(2,1)S(1)}, f32[1024,128]{1,0:T(8,128)S(1)}, f32[1024,128]{1,0:T(8,128)S(1)}) custom-call(bf16[1024,256]{1,0:T(8,128)(2,1)S(1)} %copy-done.10, bf16[1024,256]{1,0:T(8,128)(2,1)S(1)} %copy-done.6, bf16[1024,16]{1,0:T(8,128)(2,1)S(1)} %bitcast.119, ...), custom_call_target="tpu_custom_call" | custom-call | flops 3221225472 | bytes 4194304 | tf_op jit(solution)/shard_map/pallas_call | solution.py:333
  291.3 9.7 %shard_map.146 = (bf16[1024,256]{1,0:T(8,128)(2,1)S(1)}, bf16[1024,256]{1,0:T(8,128)(2,1)S(1)}, f32[1024,128]{1,0:T(8,128)S(1)}, f32[1024,128]{1,0:T(8,128)S(1)}) custom-call(bf16[1024,256]{1,0:T(8,128)(2,1)S(1)} %copy-done.9, bf16[1024,256]{1,0:T(8,128)(2,1)} %collective-permute-done.20.add_q, bf16[1024,16]{1,0:T(8,128)(2,1)S(1)} %bitcast.120, ...), custom_call_target="tpu_custom_call" | custom-call | flops 3221225472 | bytes 4194304 | tf_op jit(solution)/shard_map/pallas_call | solution.py:333
  302.7 6.4 %collective-permute-start.41 = (bf16[1024,256]{1,0:T(8,128)(2,1)S(1)}, bf16[1024,256]{1,0:T(8,128)(2,1)S(1)}, u32[]{:S(2)}, u32[]{:S(2)}) collective-permute-start(bf16[1024,256]{1,0:T(8,128)(2,1)S(1)} %add_convert_fusion.2), channel_id=1, source_target_pairs={{2,3},{1,0},{6,7},{5,4},{10,11},{9,8},{14,15},{13,12},{18,19},{17,... | collective-permute-start | bytes 1572872 | tf_op jit(solution)/shard_map/ppermute | solution.py:413
  313.1 9.7 %shard_map.147 = (bf16[1024,256]{1,0:T(8,128)(2,1)S(1)}, bf16[1024,256]{1,0:T(8,128)(2,1)S(1)}, f32[1024,128]{1,0:T(8,128)S(1)}, f32[1024,128]{1,0:T(8,128)S(1)}) custom-call(bf16[1024,256]{1,0:T(8,128)(2,1)S(1)} %copy-done.8, bf16[1024,256]{1,0:T(8,128)(2,1)} %collective-permute-done.29.add_q, bf16[1024,16]{1,0:T(8,128)(2,1)S(1)} %bitcast.121, ...), custom_call_target="tpu_custom_call" | custom-call | flops 3221225472 | bytes 4194304 | tf_op jit(solution)/shard_map/pallas_call | solution.py:333
  324.0 9.0 %shard_map.148 = (bf16[1024,256]{1,0:T(8,128)(2,1)S(1)}, bf16[1024,256]{1,0:T(8,128)(2,1)S(1)}, f32[1024,128]{1,0:T(8,128)S(1)}, f32[1024,128]{1,0:T(8,128)S(1)}) custom-call(bf16[1024,256]{1,0:T(8,128)(2,1)S(1)} %copy-done.7, bf16[1024,256]{1,0:T(8,128)(2,1)S(1)} %collective-permute-done.38.add_q, bf16[1024,16]{1,0:T(8,128)(2,1)S(1)} %bitcast.122, ...), custom_call_target="tpu_custom_call" | custom-call | flops 3221225472 | bytes 4194304 | tf_op jit(solution)/shard_map/pallas_call | solution.py:333
  358.9 6.1 %collective-permute-done.55 = f32[16,1024]{1,0:T(8,128)S(1)} collective-permute-done((f32[16,1024]{1,0:T(8,128)S(1)}, f32[16,1024]{1,0:T(8,128)S(1)}, u32[]{:S(2)}, u32[]{:S(2)}) %collective-permute-start.55) | collective-permute-done | bytes 65568 | tf_op jit(solution)/shard_map/ppermute | solution.py:432
  395.5 6.3 %collective-permute-done.46 = bf16[1024,256]{1,0:T(8,128)(2,1)S(1)} collective-permute-done((bf16[1024,256]{1,0:T(8,128)(2,1)}, bf16[1024,256]{1,0:T(8,128)(2,1)S(1)}, u32[]{:S(2)}, u32[]{:S(2)}) %collective-permute-start.46) | collective-permute-done | bytes 524320 | tf_op jit(solution)/shard_map/ppermute | solution.py:432
  403.2 9.9 %collective-permute-done.43 = bf16[1024,256]{1,0:T(8,128)(2,1)S(1)} collective-permute-done((bf16[1024,256]{1,0:T(8,128)(2,1)}, bf16[1024,256]{1,0:T(8,128)(2,1)S(1)}, u32[]{:S(2)}, u32[]{:S(2)}) %collective-permute-start.43) | collective-permute-done | bytes 524320 | tf_op jit(solution)/shard_map/ppermute | solution.py:432
  414.4 7.7 %collective-permute-done.34 = bf16[1024,256]{1,0:T(8,128)(2,1)S(1)} collective-permute-done((bf16[1024,256]{1,0:T(8,128)(2,1)}, bf16[1024,256]{1,0:T(8,128)(2,1)S(1)}, u32[]{:S(2)}, u32[]{:S(2)}) %collective-permute-start.34) | collective-permute-done | bytes 524320 | tf_op jit(solution)/shard_map/ppermute | solution.py:432
  428.0 13.2 %collective-permute-done.35 = bf16[1024,256]{1,0:T(8,128)(2,1)S(1)} collective-permute-done((bf16[1024,256]{1,0:T(8,128)(2,1)S(1)}, bf16[1024,256]{1,0:T(8,128)(2,1)S(1)}, u32[]{:S(2)}, u32[]{:S(2)}) %collective-permute-start.35) | collective-permute-done | bytes 524320 | tf_op jit(solution)/shard_map/ppermute | solution.py:432
  455.6 6.6 %fusion = f32[1024,1024]{1,0:T(8,128)S(1)} fusion(bf16[1024,2048]{1,0:T(8,128)(2,1)S(1)} %select_dynamic-update-slice_fusion, bf16[2048,2048]{1,0:T(8,128)(2,1)} %param.12), kind=kOutput, calls=%fused_computation.1 | convolution fusion | flops 4294967296 | bytes 12582912 | tf_op jit(solution)/shard_map/dot_general | solution.py:41
  468.4 5.6 %collective-permute-done.53 = f32[48,1024]{1,0:T(8,128)S(1)} collective-permute-done((f32[48,1024]{1,0:T(8,128)S(1)}, f32[48,1024]{1,0:T(8,128)S(1)}, u32[]{:S(2)}, u32[]{:S(2)}) %collective-permute-start.53) | collective-permute-done | bytes 196640 | tf_op jit(solution)/shard_map/ppermute | solution.py:24
  478.7 10.6 %collective-permute-done.49 = bf16[256,1024]{1,0:T(8,128)(2,1)S(1)} collective-permute-done((bf16[256,1024]{1,0:T(8,128)(2,1)S(1)}, bf16[256,1024]{1,0:T(8,128)(2,1)S(1)}, u32[]{:S(2)}, u32[]{:S(2)}) %collective-permute-start.49) | collective-permute-done | bytes 524320 | tf_op jit(solution)/shard_map/ppermute | solution.py:24
  489.5 9.7 %collective-permute-done.51 = bf16[256,1024]{1,0:T(8,128)(2,1)S(1)} collective-permute-done((bf16[256,1024]{1,0:T(8,128)(2,1)S(1)}, bf16[256,1024]{1,0:T(8,128)(2,1)S(1)}, u32[]{:S(2)}, u32[]{:S(2)}) %collective-permute-start.51) | collective-permute-done | bytes 524320 | tf_op jit(solution)/shard_map/ppermute | solution.py:24
  (293 shorter events, 269.6 us)
Async XLA Ops:
  7.2 38.0 %all-gather.3.cloned.1.call-start = ((), (), s32[]{:S(2)}) async-start(), calls=%async_computation | async-start | bytes 5242880 | tf_op jit(solution)/shard_map/all_gather | solution.py:394
  7.9 158.0 %all-gather.5.cloned.1.call-start = ((), (), s32[]{:S(2)}) async-start(), calls=%async_computation.1 | async-start | bytes 5242880 | tf_op jit(solution)/shard_map/all_gather | solution.py:396
  59.2 40.8 %collective-permute-start.12 = (bf16[1024,256]{1,0:T(8,128)(2,1)}, bf16[1024,256]{1,0:T(8,128)(2,1)}, u32[]{:S(2)}, u32[]{:S(2)}) collective-permute-start(bf16[1024,256]{1,0:T(8,128)(2,1)} %broadcast_select_fusion.6), channel_id=1, source_target_pairs={{0,1},{3,2},{4,5},{7,6},{8,9},{11,10},{12,13},{15,14},{16,17},{19,... | collective-permute-start | bytes 1572872 | tf_op jit(solution)/shard_map/ppermute | solution.py:413
  68.4 35.4 %collective-permute-start.18 = (bf16[1024,256]{1,0:T(8,128)(2,1)}, bf16[1024,256]{1,0:T(8,128)(2,1)}, u32[]{:S(2)}, u32[]{:S(2)}) collective-permute-start(bf16[1024,256]{1,0:T(8,128)(2,1)} %get-tuple-element.58), channel_id=1, source_target_pairs={{0,1},{3,2},{4,5},{7,6},{8,9},{11,10},{12,13},{15,14},{16,17},{19,... | collective-permute-start | bytes 1572872 | tf_op jit(solution)/shard_map/ppermute | solution.py:413
  74.6 33.9 %collective-permute-start = (bf16[1024,256]{1,0:T(8,128)(2,1)S(1)}, bf16[1024,256]{1,0:T(8,128)(2,1)S(1)}, u32[]{:S(2)}, u32[]{:S(2)}) collective-permute-start(bf16[1024,256]{1,0:T(8,128)(2,1)S(1)} %get-tuple-element.62), channel_id=1, source_target_pairs={{0,1},{3,2},{4,5},{7,6},{8,9},{11,10},{12,13},{15,14},{16,17},{19,... | collective-permute-start | bytes 1572872 | tf_op jit(solution)/shard_map/ppermute | solution.py:413
  101.3 28.2 %collective-permute-start.13 = (bf16[1024,256]{1,0:T(8,128)(2,1)S(1)}, bf16[1024,256]{1,0:T(8,128)(2,1)S(1)}, u32[]{:S(2)}, u32[]{:S(2)}) collective-permute-start(bf16[1024,256]{1,0:T(8,128)(2,1)S(1)} %add_convert_fusion.15), channel_id=1, source_target_pairs={{1,2},{2,1},{5,6},{6,5},{9,10},{10,9},{13,14},{14,13},{17,18},{18,... | collective-permute-start | bytes 1572872 | tf_op jit(solution)/shard_map/ppermute | solution.py:413
  108.7 31.8 %collective-permute-start.1 = (bf16[1024,256]{1,0:T(8,128)(2,1)S(1)}, bf16[1024,256]{1,0:T(8,128)(2,1)S(1)}, u32[]{:S(2)}, u32[]{:S(2)}) collective-permute-start(bf16[1024,256]{1,0:T(8,128)(2,1)S(1)} %add_convert_fusion.19), channel_id=1, source_target_pairs={{1,2},{2,1},{5,6},{6,5},{9,10},{10,9},{13,14},{14,13},{17,18},{18,... | collective-permute-start | bytes 1572872 | tf_op jit(solution)/shard_map/ppermute | solution.py:413
  115.7 36.1 %collective-permute-start.28 = (bf16[1024,256]{1,0:T(8,128)(2,1)S(1)}, bf16[1024,256]{1,0:T(8,128)(2,1)S(1)}, u32[]{:S(2)}, u32[]{:S(2)}) collective-permute-start(bf16[1024,256]{1,0:T(8,128)(2,1)S(1)} %add_convert_fusion.9), channel_id=1, source_target_pairs={{1,2},{2,1},{5,6},{6,5},{9,10},{10,9},{13,14},{14,13},{17,18},{18,... | collective-permute-start | bytes 1572872 | tf_op jit(solution)/shard_map/ppermute | solution.py:413
  126.2 33.3 %collective-permute-start.37 = (bf16[1024,256]{1,0:T(8,128)(2,1)S(1)}, bf16[1024,256]{1,0:T(8,128)(2,1)S(1)}, u32[]{:S(2)}, u32[]{:S(2)}) collective-permute-start(bf16[1024,256]{1,0:T(8,128)(2,1)S(1)} %add_convert_fusion.5), channel_id=1, source_target_pairs={{1,2},{2,1},{5,6},{6,5},{9,10},{10,9},{13,14},{14,13},{17,18},{18,... | collective-permute-start | bytes 1572872 | tf_op jit(solution)/shard_map/ppermute | solution.py:413
  129.8 30.7 %collective-permute-start.14 = (bf16[1024,256]{1,0:T(8,128)(2,1)S(1)}, bf16[1024,256]{1,0:T(8,128)(2,1)S(1)}, u32[]{:S(2)}, u32[]{:S(2)}) collective-permute-start(bf16[1024,256]{1,0:T(8,128)(2,1)S(1)} %add_convert_fusion.14), channel_id=1, source_target_pairs={{2,3},{1,0},{6,7},{5,4},{10,11},{9,8},{14,15},{13,12},{18,19},{17,... | collective-permute-start | bytes 1572872 | tf_op jit(solution)/shard_map/ppermute | solution.py:413
  132.2 154.1 %collective-permute-start.20 = (bf16[1024,256]{1,0:T(8,128)(2,1)}, bf16[1024,256]{1,0:T(8,128)(2,1)}, u32[]{:S(2)}, u32[]{:S(2)}) collective-permute-start(bf16[1024,256]{1,0:T(8,128)(2,1)} %add_convert_fusion.12), channel_id=1, source_target_pairs={{2,3},{1,0},{6,7},{5,4},{10,11},{9,8},{14,15},{13,12},{18,19},{17,... | collective-permute-start | bytes 1572872 | tf_op jit(solution)/shard_map/ppermute | solution.py:413
  141.5 125.6 %collective-permute-start.2 = (bf16[1024,256]{1,0:T(8,128)(2,1)}, bf16[1024,256]{1,0:T(8,128)(2,1)S(1)}, u32[]{:S(2)}, u32[]{:S(2)}) collective-permute-start(bf16[1024,256]{1,0:T(8,128)(2,1)} %add_convert_fusion.18), channel_id=1, source_target_pairs={{2,3},{1,0},{6,7},{5,4},{10,11},{9,8},{14,15},{13,12},{18,19},{17,... | collective-permute-start | bytes 1572872 | tf_op jit(solution)/shard_map/ppermute | solution.py:413
  152.8 149.8 %collective-permute-start.29 = (bf16[1024,256]{1,0:T(8,128)(2,1)}, bf16[1024,256]{1,0:T(8,128)(2,1)}, u32[]{:S(2)}, u32[]{:S(2)}) collective-permute-start(bf16[1024,256]{1,0:T(8,128)(2,1)} %add_convert_fusion.8), channel_id=1, source_target_pairs={{2,3},{1,0},{6,7},{5,4},{10,11},{9,8},{14,15},{13,12},{18,19},{17,... | collective-permute-start | bytes 1572872 | tf_op jit(solution)/shard_map/ppermute | solution.py:413
  174.0 36.0 %collective-permute-start.21 = (bf16[1024,256]{1,0:T(8,128)(2,1)}, bf16[1024,256]{1,0:T(8,128)(2,1)}, u32[]{:S(2)}, u32[]{:S(2)}) collective-permute-start(bf16[1024,256]{1,0:T(8,128)(2,1)} %get-tuple-element.56), channel_id=1, source_target_pairs={{0,1},{3,2},{4,5},{7,6},{8,9},{11,10},{12,13},{15,14},{16,17},{19,... | collective-permute-start | bytes 1572872 | tf_op jit(solution)/shard_map/ppermute | solution.py:413
  268.0 41.2 %collective-permute-start.38 = (bf16[1024,256]{1,0:T(8,128)(2,1)S(1)}, bf16[1024,256]{1,0:T(8,128)(2,1)S(1)}, u32[]{:S(2)}, u32[]{:S(2)}) collective-permute-start(bf16[1024,256]{1,0:T(8,128)(2,1)S(1)} %copy-done.25), channel_id=1, source_target_pairs={{2,3},{1,0},{6,7},{5,4},{10,11},{9,8},{14,15},{13,12},{18,19},{17,... | collective-permute-start | bytes 1572872 | tf_op jit(solution)/shard_map/ppermute | solution.py:413
  273.6 27.4 %collective-permute-start.40 = (bf16[1024,256]{1,0:T(8,128)(2,1)S(1)}, bf16[1024,256]{1,0:T(8,128)(2,1)S(1)}, u32[]{:S(2)}, u32[]{:S(2)}) collective-permute-start(bf16[1024,256]{1,0:T(8,128)(2,1)S(1)} %add_convert_fusion.3), channel_id=1, source_target_pairs={{1,2},{2,1},{5,6},{6,5},{9,10},{10,9},{13,14},{14,13},{17,18},{18,... | collective-permute-start | bytes 1572872 | tf_op jit(solution)/shard_map/ppermute | solution.py:413
  350.4 29.3 %collective-permute-start.42 = (bf16[1024,256]{1,0:T(8,128)(2,1)S(1)}, bf16[1024,256]{1,0:T(8,128)(2,1)}, u32[]{:S(2)}, u32[]{:S(2)}) collective-permute-start(bf16[1024,256]{1,0:T(8,128)(2,1)S(1)} %get-tuple-element.33), channel_id=1, source_target_pairs={{0,1},{3,2},{4,5},{7,6},{8,9},{11,10},{12,13},{15,14},{16,17},{19,... | collective-permute-start | bytes 1572872 | tf_op jit(solution)/shard_map/ppermute | solution.py:432
  351.7 30.3 %collective-permute-start.33 = (bf16[1024,256]{1,0:T(8,128)(2,1)S(1)}, bf16[1024,256]{1,0:T(8,128)(2,1)}, u32[]{:S(2)}, u32[]{:S(2)}) collective-permute-start(bf16[1024,256]{1,0:T(8,128)(2,1)S(1)} %get-tuple-element.31), channel_id=1, source_target_pairs={{0,1},{3,2},{4,5},{7,6},{8,9},{11,10},{12,13},{15,14},{16,17},{19,... | collective-permute-start | bytes 1572872 | tf_op jit(solution)/shard_map/ppermute | solution.py:432
  353.0 32.5 %collective-permute-start.16 = (bf16[1024,256]{1,0:T(8,128)(2,1)}, bf16[1024,256]{1,0:T(8,128)(2,1)}, u32[]{:S(2)}, u32[]{:S(2)}) collective-permute-start(bf16[1024,256]{1,0:T(8,128)(2,1)} %collective-permute-done.15), channel_id=1, source_target_pairs={{1,2},{2,1},{5,6},{6,5},{9,10},{10,9},{13,14},{14,13},{17,18},{18,... | collective-permute-start | bytes 1572872 | tf_op jit(solution)/shard_map/ppermute | solution.py:432
  379.6 33.4 %collective-permute-start.43 = (bf16[1024,256]{1,0:T(8,128)(2,1)}, bf16[1024,256]{1,0:T(8,128)(2,1)S(1)}, u32[]{:S(2)}, u32[]{:S(2)}) collective-permute-start(bf16[1024,256]{1,0:T(8,128)(2,1)} %collective-permute-done.42), channel_id=1, source_target_pairs={{1,2},{2,1},{5,6},{6,5},{9,10},{10,9},{13,14},{14,13},{17,18},{18,... | collective-permute-start | bytes 1572872 | tf_op jit(solution)/shard_map/ppermute | solution.py:432
  382.0 40.2 %collective-permute-start.34 = (bf16[1024,256]{1,0:T(8,128)(2,1)}, bf16[1024,256]{1,0:T(8,128)(2,1)S(1)}, u32[]{:S(2)}, u32[]{:S(2)}) collective-permute-start(bf16[1024,256]{1,0:T(8,128)(2,1)} %collective-permute-done.33), channel_id=1, source_target_pairs={{1,2},{2,1},{5,6},{6,5},{9,10},{10,9},{13,14},{14,13},{17,18},{18,... | collective-permute-start | bytes 1572872 | tf_op jit(solution)/shard_map/ppermute | solution.py:432
  385.5 38.1 %collective-permute-start.17 = (bf16[1024,256]{1,0:T(8,128)(2,1)}, bf16[1024,256]{1,0:T(8,128)(2,1)S(1)}, u32[]{:S(2)}, u32[]{:S(2)}) collective-permute-start(bf16[1024,256]{1,0:T(8,128)(2,1)} %collective-permute-done.16), channel_id=1, source_target_pairs={{2,3},{1,0},{6,7},{5,4},{10,11},{9,8},{14,15},{13,12},{18,19},{17,... | collective-permute-start | bytes 1572872 | tf_op jit(solution)/shard_map/ppermute | solution.py:432
  390.7 34.2 %collective-permute-start.26 = (bf16[1024,256]{1,0:T(8,128)(2,1)}, bf16[1024,256]{1,0:T(8,128)(2,1)S(1)}, u32[]{:S(2)}, u32[]{:S(2)}) collective-permute-start(bf16[1024,256]{1,0:T(8,128)(2,1)} %collective-permute-done.25), channel_id=1, source_target_pairs={{2,3},{1,0},{6,7},{5,4},{10,11},{9,8},{14,15},{13,12},{18,19},{17,... | collective-permute-start | bytes 1572872 | tf_op jit(solution)/shard_map/ppermute | solution.py:432
  413.1 30.5 %collective-permute-start.44 = (bf16[1024,256]{1,0:T(8,128)(2,1)S(1)}, bf16[1024,256]{1,0:T(8,128)(2,1)S(1)}, u32[]{:S(2)}, u32[]{:S(2)}) collective-permute-start(bf16[1024,256]{1,0:T(8,128)(2,1)S(1)} %collective-permute-done.43), channel_id=1, source_target_pairs={{2,3},{1,0},{6,7},{5,4},{10,11},{9,8},{14,15},{13,12},{18,19},{17,... | collective-permute-start | bytes 1572872 | tf_op jit(solution)/shard_map/ppermute | solution.py:432
  (72 other events, 1213.5 us)
Sparse Core Ops, SparseCore 0:
  9.5 35.5 all-gather.2
  69.9 37.2 all-gather.4
